TPU v7x, 32 devices: a whole 2x2x4 slice. The times are simulated.
32 devices in a mesh: gz: 32 (over z, y, x, core).
Axes of the slice: x: 2, y: 2, z: 4, core: 2. Of those that a mesh axis runs over, the one named last changes fastest.
Arguments:
- right_side: float32 [64, 512, 512], P('gz'), may hold values from -20 to 20
- cell_flags: int32 [64, 512, 512], P('gz'), may hold values from 0 to 2
Outputs:
- solution: float32 [64, 512, 512], P('gz')
- residual: float32 [64, 512, 512], P('gz')
All inputs are finite; a program needn't handle non-finite values.
Results may differ from a plain program's by a relative error of at most 0.00011.
Values sent between devices are 32-bit elements; how exact they have to be, the bound alone decides.
A program may use at most 128 MiB of HBM per device.

v0:
```python
import functools
import math

import jax
import jax.numpy as jnp
from jax import lax
from jax.experimental import pallas as pl
from jax.experimental.pallas import tpu as pltpu
from jax.sharding import PartitionSpec as P

MESH = pl.DeviceIdType.MESH
TILE = 16
PAD = 8
AHEAD = 2
VMEM_BYTES = 67_043_328


def kernel(
    count, near, chunk,
    side_hbm, flag_hbm, sol_ref, res_ref,
    rhs, flags, r0, inv, solid, u0, u1, w0, w1, halo_r, halo_u, bits_out, bits_in,
    mine, near_got, far_got,
    in_sem, bit_send, bit_recv, halo_send, halo_recv,
    near_send, near_recv, far_send, far_recv,
):
    depth, rows, cols = rhs.shape
    words = rows // 32
    chunks = rows // chunk
    tiles = chunk // TILE
    far = count // near
    me = lax.axis_index("gz")
    low, high = lax.rem(me, near), me // near
    first_side = 1 - lax.rem(me, 2)

    def load(plane, which):
        source, target = ((flag_hbm, flags), (side_hbm, rhs))[which]
        return pltpu.make_async_copy(source.at[plane], target.at[plane], in_sem.at[which, plane])

    for plane in range(depth):
        for which in range(2):
            load(plane, which).start()

    def present(side):
        return jnp.where(side == 0, me > 0, me < count - 1)

    def neighbour(side):
        return me - 1 + 2 * side

    near_ids = [high * near + lax.rem(low + j, near) for j in range(1, near)]
    far_ids = [lax.rem(high + j, far) * near + low for j in range(1, far)]
    barrier = pltpu.get_barrier_semaphore()
    for other in near_ids + far_ids:
        pl.semaphore_signal(barrier, inc=1, device_id=(other,), device_id_type=MESH)
    outside = (
        jnp.logical_and(low == 0, me > 0),
        jnp.logical_and(low == near - 1, me < count - 1),
    )
    for side in range(2):
        @pl.when(outside[side])
        def _():
            pl.semaphore_signal(barrier, inc=1, device_id=(neighbour(side),), device_id_type=MESH)

    blank = jnp.zeros((PAD, cols), jnp.float32)
    for ref in (u0, u1, solid):
        for plane in range(ref.shape[0]):
            ref[plane, 0:PAD, :] = blank
            ref[plane, rows + PAD:rows + 2 * PAD, :] = blank
    for side in range(2):
        @pl.when(jnp.logical_not(present(side)))
        def _():
            bits_in[side] = jnp.zeros((2, words, cols), jnp.int32)

            def clear(t, carry):
                at = pl.ds(pl.multiple_of(t * TILE, TILE), TILE)
                halo_r[side, at, :] = jnp.zeros((TILE, cols), jnp.float32)
                halo_u[side, at, :] = jnp.zeros((TILE, cols), jnp.float32)
                return carry

            lax.fori_loop(0, rows // TILE, clear, 0)

    def halo_copy(phase, side, k):
        at = pl.multiple_of(k * chunk, chunk)
        plane = side * (depth - 1)
        if phase == 0:
            source, target = r0.at[plane, pl.ds(at, chunk)], halo_r
        else:
            source, target = u1.at[plane, pl.ds(pl.multiple_of(at + PAD, PAD), chunk)], halo_u
        return pltpu.make_async_remote_copy(
            src_ref=source,
            dst_ref=target.at[1 - side, pl.ds(at, chunk)],
            send_sem=halo_send.at[phase, side, k],
            recv_sem=halo_recv.at[phase, 1 - side, k],
            device_id=(neighbour(side),),
            device_id_type=MESH,
        )

    def halo_arrival(phase, side, k):
        at = pl.multiple_of(k * chunk, chunk)
        target = halo_r if phase == 0 else halo_u
        return pltpu.make_async_remote_copy(
            src_ref=target.at[side, pl.ds(at, chunk)],
            dst_ref=target.at[side, pl.ds(at, chunk)],
            send_sem=halo_send.at[phase, side, k],
            recv_sem=halo_recv.at[phase, side, k],
            device_id=(neighbour(side),),
            device_id_type=MESH,
        )

    def send_halo(phase, side, k):
        @pl.when(present(side))
        def _():
            halo_copy(phase, side, k).start()

    def wait_halo(phase, side, k):
        @pl.when(present(side))
        def _():
            halo_arrival(phase, side, k).wait_recv()

    def row(k, t):
        return pl.multiple_of(k * chunk + t * TILE, TILE)

    for plane in range(depth):
        load(plane, 0).wait()
        load(plane, 1).wait()
    edge_first = [0, depth - 1] + list(range(1, depth - 1))

    def mask_rows(k):
        for plane in edge_first:
            def mask_tile(t, carry, plane=plane):
                at = pl.ds(row(k, t), TILE)
                r0[plane, at, :] = jnp.where(flags[plane, at, :] == 1, rhs[plane, at, :], 0.0)
                return carry

            lax.fori_loop(0, tiles, mask_tile, 0)

    def send_both(phase, k):
        for side in range(2):
            send_halo(phase, side, k)

    def mask_chunk(k, carry):
        mask_rows(k)
        send_both(0, k)
        return carry

    mask_rows(0)
    peers = near + far - 2 + outside[0].astype(jnp.int32) + outside[1].astype(jnp.int32)
    pl.semaphore_wait(barrier, peers)

    send_both(0, 0)

    outer = sorted({0, 1, depth - 2, depth - 1})
    for plane in range(depth):

        def pack(j, word, plane=plane):
            at = pl.ds(pl.multiple_of(j * words, words), words)
            is_solid = flags[plane, at, :] == 2
            padded = pl.ds(pl.multiple_of(j * words + PAD, PAD), words)
            solid[plane + 2, padded, :] = jnp.where(is_solid, 1.0, 0.0)
            return word | jnp.left_shift(jnp.where(is_solid, 1, 0), j)

        word = lax.fori_loop(0, 32, pack, jnp.zeros((words, cols), jnp.int32))
        if plane in outer:
            bits_out[outer.index(plane)] = word

    def bit_copy(side):
        lead = 0 if side == 0 else len(outer) - 2
        return pltpu.make_async_remote_copy(
            src_ref=bits_out.at[pl.ds(lead, 2)],
            dst_ref=bits_in.at[1 - side],
            send_sem=bit_send.at[side],
            recv_sem=bit_recv.at[1 - side],
            device_id=(neighbour(side),),
            device_id_type=MESH,
        )

    for side in range(2):
        @pl.when(present(side))
        def _():
            bit_copy(side).start()

    lax.fori_loop(1, chunks, mask_chunk, 0)

    for side in range(2):
        @pl.when(present(side))
        def _():
            bit_copy(1 - side).wait_recv()
        for i in range(2):
            def unpack(j, carry, side=side, i=i):
                padded = pl.ds(pl.multiple_of(j * words + PAD, PAD), words)
                bit = jnp.bitwise_and(jnp.right_shift(bits_in[side, i], j), 1)
                solid[side * (depth + 2) + i, padded, :] = bit.astype(jnp.float32)
                return carry

            lax.fori_loop(0, 32, unpack, 0)

    column = lax.broadcasted_iota(jnp.int32, (TILE, cols), 1)

    def inplane(ref, plane, start):
        block = ref[plane, pl.ds(start, TILE + 2 * PAD), :]
        centre = block[PAD:PAD + TILE]
        total = block[PAD - 1:PAD - 1 + TILE] + block[PAD + 1:PAD + 1 + TILE]
        total = total + jnp.where(column == 0, 0.0, pltpu.roll(centre, 1, 1))
        total = total + jnp.where(column == cols - 1, 0.0, pltpu.roll(centre, cols - 1, 1))
        return centre, total

    def centre_of(ref, plane, start):
        return ref[plane, pl.ds(pl.multiple_of(start + PAD, PAD), TILE), :]

    def put(ref, plane, start, value):
        ref[plane, pl.ds(pl.multiple_of(start + PAD, PAD), TILE), :] = value

    def fold(value):
        total = value[0:8]
        for i in range(8, TILE, 8):
            total = total + value[i:i + 8]
        return total

    none = jnp.zeros((8, cols), jnp.float32)
    steps = rows // TILE

    def inverse(plane, start):
        _, total = inplane(solid, plane + 1, start)
        total = total + centre_of(solid, plane, start) + centre_of(solid, plane + 2, start)
        return 1.0 / jnp.maximum(6.0 - total, 1.0)

    def first(t, rz):
        start = pl.multiple_of(t * TILE, TILE)
        at = pl.ds(start, TILE)
        for plane in range(depth):
            value = jnp.where(flags[plane, at, :] == 1, inverse(plane + 1, start), 0.0)
            inv[plane + 1, at, :] = value
            residual = r0[plane, at, :]
            precond = residual * value
            put(u0, plane, start, precond)
            rz = rz + fold(residual * precond)
        for plane in (0, depth + 1):
            inv[plane, at, :] = inverse(plane, start)
        return rz

    rz = lax.fori_loop(0, steps, first, none)

    def local_part(field, scaled, out, plane, start):
        at = pl.ds(start, TILE)
        _, total = inplane(field, plane, start)
        if plane > 0:
            total = total + centre_of(field, plane - 1, start)
        if plane < depth - 1:
            total = total + centre_of(field, plane + 1, start)
        image = jnp.where(inv[plane + 1, at, :] > 0.0, scaled[plane, at, :] - total, 0.0)
        out[plane, at, :] = image
        return image

    def second(t, inner):
        start = pl.multiple_of(t * TILE, TILE)
        for plane in range(depth):
            image = local_part(u0, r0, w0, plane, start)
            if 0 < plane < depth - 1:
                put(u1, plane, start, image * inv[plane + 1, pl.ds(start, TILE), :])
                inner = inner + fold(image * centre_of(u0, plane, start))
        return inner

    inner = lax.fori_loop(0, steps, second, none)

    def edge_one(side, inner, ahead):
        plane = side * (depth - 1)

        def step(k, inner):
            wait_halo(0, side, k)

            def tile(t, inner):
                start = row(k, t)
                at = pl.ds(start, TILE)
                value = inv[plane + 1, at, :]
                beyond = halo_r[side, at, :] * inv[side * (depth + 1), at, :]
                image = jnp.where(value > 0.0, w0[plane, at, :] - beyond, 0.0)
                w0[plane, at, :] = image
                put(u1, plane, start, image * value)
                return inner + fold(image * centre_of(u0, plane, start))

            inner = lax.fori_loop(0, tiles, tile, inner)

            @pl.when(k < ahead)
            def _():
                send_halo(1, side, k)

            return inner

        return lax.fori_loop(0, chunks, step, inner)

    inner = edge_one(first_side, inner, chunks)
    inner = edge_one(1 - first_side, inner, AHEAD)

    def lanes(value):
        total = value[:, 0:128]
        for i in range(128, cols, 128):
            total = total + value[:, i:i + 128]
        return total

    def near_copy(turn, j):
        return pltpu.make_async_remote_copy(
            src_ref=mine.at[turn, 0],
            dst_ref=near_got.at[turn, low],
            send_sem=near_send.at[turn, j],
            recv_sem=near_recv.at[turn, low],
            device_id=(near_ids[j - 1],),
            device_id_type=MESH,
        )

    def far_copy(turn, j):
        return pltpu.make_async_remote_copy(
            src_ref=mine.at[turn, 1],
            dst_ref=far_got.at[turn, high],
            send_sem=far_send.at[turn, j],
            recv_sem=far_recv.at[turn, high],
            device_id=(far_ids[j - 1],),
            device_id_type=MESH,
        )

    def sum_start(turn, one, two):
        mine[turn, 0, 0] = lanes(one)
        mine[turn, 0, 1] = lanes(two)
        for j in range(1, near):
            near_copy(turn, j).start()

    def arrived(turn, got, slot, send, recv, other):
        return pltpu.make_async_remote_copy(
            src_ref=got.at[turn, slot],
            dst_ref=got.at[turn, slot],
            send_sem=send.at[turn, 0],
            recv_sem=recv.at[turn, slot],
            device_id=(other,),
            device_id_type=MESH,
        )

    def sum_middle(turn):
        near_got[turn, low] = mine[turn, 0]
        for j in range(1, near):
            slot = lax.rem(low + j, near)
            arrived(turn, near_got, slot, near_send, near_recv, near_ids[j - 1]).wait_recv()
        total = near_got[turn, 0]
        for i in range(1, near):
            total = total + near_got[turn, i]
        mine[turn, 1] = total
        for j in range(1, far):
            far_copy(turn, j).start()

    def sum_end(turn):
        far_got[turn, high] = mine[turn, 1]
        for j in range(1, far):
            slot = lax.rem(high + j, far)
            arrived(turn, far_got, slot, far_send, far_recv, far_ids[j - 1]).wait_recv()
        total = far_got[turn, 0]
        for i in range(1, far):
            total = total + far_got[turn, i]
        return (
            jnp.sum(total[0], keepdims=True),
            jnp.sum(total[1], keepdims=True),
        )

    sum_start(0, rz, inner)

    def send_rest(k, carry):
        send_halo(1, 1 - first_side, k)
        return carry

    lax.fori_loop(AHEAD, chunks, send_rest, 0)

    def third(t, carry):
        start = pl.multiple_of(t * TILE, TILE)
        for plane in range(depth):
            local_part(u1, w0, w1, plane, start)
        return carry

    half = steps // 2
    lax.fori_loop(0, half, third, 0)
    sum_middle(0)
    lax.fori_loop(half, steps, third, 0)
    rz_old, product = sum_end(0)
    step_old = rz_old / product

    def contribution(plane, start, image, carry):
        at = pl.ds(start, TILE)
        along = w0[plane, at, :]
        residual = r0[plane, at, :] - step_old * along
        precond = centre_of(u0, plane, start) - step_old * centre_of(u1, plane, start)
        applied = along - step_old * image
        return (
            carry[0] + fold(residual * precond),
            carry[1] + fold(applied * precond),
        )

    carry = (none, none)
    for plane in range(1, depth - 1):
        def whole(t, carry, plane=plane):
            start = pl.multiple_of(t * TILE, TILE)
            return contribution(plane, start, w1[plane, pl.ds(start, TILE), :], carry)

        carry = lax.fori_loop(0, steps, whole, carry)

    def edge_two(side, carry):
        plane = side * (depth - 1)

        def step(k, carry):
            wait_halo(1, side, k)

            def tile(t, carry):
                start = row(k, t)
                at = pl.ds(start, TILE)
                image = w1[plane, at, :] - halo_u[side, at, :]
                image = jnp.where(inv[plane + 1, at, :] > 0.0, image, 0.0)
                w1[plane, at, :] = image
                return contribution(plane, start, image, carry)

            return lax.fori_loop(0, tiles, tile, carry)

        return lax.fori_loop(0, chunks, step, carry)

    carry = edge_two(first_side, carry)
    carry = edge_two(1 - first_side, carry)
    sum_start(1, *carry)
    sum_middle(1)
    rz_now, product = sum_end(1)
    blend = rz_now / rz_old
    step_size = rz_now / (product - blend * rz_now / step_old)

    for plane in range(depth):
        def last(t, carry, plane=plane):
            start = pl.multiple_of(t * TILE, TILE)
            at = pl.ds(start, TILE)
            direction = centre_of(u0, plane, start)
            along = w0[plane, at, :]
            precond = direction - step_old * centre_of(u1, plane, start)
            applied = along - step_old * w1[plane, at, :]
            residual = r0[plane, at, :] - step_old * along
            sol_ref[plane, at, :] = step_old * direction + step_size * (precond + blend * direction)
            res_ref[plane, at, :] = residual - step_size * (applied + blend * along)
            return carry

        lax.fori_loop(0, steps, last, 0)

    for side in range(2):
        @pl.when(present(side))
        def _():
            bit_copy(side).wait_send()
            for phase in range(2):
                for k in range(chunks):
                    halo_copy(phase, side, k).wait_send()
    for turn in range(2):
        for j in range(1, near):
            near_copy(turn, j).wait_send()
        for j in range(1, far):
            far_copy(turn, j).wait_send()


def body(count, right_side, cell_flags):
    depth, rows, cols = right_side.shape
    near = math.gcd(count, 8)
    far = count // near
    chunk = math.gcd(rows, 64)
    chunks = rows // chunk
    f32 = jnp.float32
    field = pltpu.VMEM((depth, rows, cols), f32)
    padded = pltpu.VMEM((depth, rows + 2 * PAD, cols), f32)
    outer = len({0, 1, depth - 2, depth - 1})
    dma = pltpu.SemaphoreType.DMA
    grant = VMEM_BYTES - 8 * right_side.size - 2**19
    return pl.pallas_call(
        functools.partial(kernel, count, near, chunk),
        out_shape=(field, field),
        in_specs=[pl.BlockSpec(memory_space=pltpu.HBM)] * 2,
        out_specs=(pl.BlockSpec(memory_space=pltpu.VMEM),) * 2,
        scratch_shapes=[
            field,
            pltpu.VMEM((depth, rows, cols), jnp.int32),
            field,
            pltpu.VMEM((depth + 2, rows, cols), f32),
            pltpu.VMEM((depth + 4, rows + 2 * PAD, cols), f32),
            padded, padded, field, field,
            pltpu.VMEM((2, rows, cols), f32),
            pltpu.VMEM((2, rows, cols), f32),
            pltpu.VMEM((outer, rows // 32, cols), jnp.int32),
            pltpu.VMEM((2, 2, rows // 32, cols), jnp.int32),
            pltpu.VMEM((2, 2, 2, 8, 128), f32),
            pltpu.VMEM((2, near, 2, 8, 128), f32),
            pltpu.VMEM((2, far, 2, 8, 128), f32),
            dma((2, depth)),
            dma((2,)), dma((2,)),
            dma((2, 2, chunks)), dma((2, 2, chunks)),
            dma((2, near)), dma((2, near)),
            dma((2, far)), dma((2, far)),
        ],
        compiler_params=pltpu.CompilerParams(
            collective_id=0, has_side_effects=True, vmem_limit_bytes=grant
        ),
    )(right_side, cell_flags)


def solution(mesh):
    placed = (P("gz", None, None), P("gz", None, None))
    return jax.shard_map(
        functools.partial(body, mesh.shape["gz"]),
        mesh=mesh,
        in_specs=placed,
        out_specs=placed,
        check_vma=False,
    )
```

profile of v0, /device:TPU:1, one launch (start us, length us, event | category | flops | bytes accessed | tf_op | source)
XLA Modules:
  0.0 66.2 jit_solution(11676842012484414083)
XLA Ops:
  0.6 62.9 %shard_map.41 = (f32[2,512,512]{2,1,0:T(8,128)S(1)}, f32[2,512,512]{2,1,0:T(8,128)S(1)}) custom-call(f32[2,512,512]{2,1,0:T(8,128)} %side_hbm.1, s32[2,512,512]{2,1,0:T(8,128)} %flag_hbm.1), custom_call_target="tpu_custom_call" | custom-call | tf_op jit(solution)/shard_map/pallas_call | solution.py:467
  63.6 1.3 %copy.6 = f32[2,512,512]{2,1,0:T(8,128)} copy(f32[2,512,512]{2,1,0:T(8,128)S(1)} %get-tuple-element.2) | data formatting | bytes 4194304
  64.9 1.3 %copy.7 = f32[2,512,512]{2,1,0:T(8,128)} copy(f32[2,512,512]{2,1,0:T(8,128)S(1)} %get-tuple-element.3) | data formatting | bytes 4194304
where the time goes:
time: 67.5 us; the launch traced here: 66.2 us
  Pallas kernels  62.9 us (93%)
  local copies, waits for them, and re-layouts  2.64 us (4%)
    pallas_call x1, Pallas kernels, body(): pl.pallas_call(functools.partial(kernel, count, near, chunk), out_shape=(...  62.9 us
    unnamed x2, local copies, waits for them, and re-layouts  2.64 us

commit v1 on v0

v1 whole, which is shorter than its diff:
```python
import functools
import math

import jax
import jax.numpy as jnp
from jax import lax
from jax.experimental import pallas as pl
from jax.experimental.pallas import tpu as pltpu
from jax.sharding import PartitionSpec as P

MESH = pl.DeviceIdType.MESH
TILE = 16
PAD = 8
VMEM_BYTES = 67_043_328


def kernel(
    count, chunk, stages,
    side_hbm, flag_hbm, sol_ref, res_ref,
    rhs, flags, r0, inv, solid, u0, u1, w0, w1, halo_r, halo_u, bits_out, bits_in,
    pair, totals, mine, got,
    in_sem, bit_send, bit_recv, halo_send, halo_recv,
    pair_send, pair_recv, total_send, total_recv, sum_send, sum_recv,
):
    depth, rows, cols = rhs.shape
    words = rows // 32
    chunks = rows // chunk
    tiles = chunk // TILE
    me = lax.axis_index("gz")
    chip, odd = me // 2, lax.rem(me, 2)
    near_side, far_side = 1 - odd, odd
    partner = me + 1 - 2 * odd

    def load(plane, which):
        source, target = ((flag_hbm, flags), (side_hbm, rhs))[which]
        return pltpu.make_async_copy(source.at[plane], target.at[plane], in_sem.at[which, plane])

    def present(side):
        return jnp.where(side == 0, me > 0, me < count - 1)

    def neighbour(side):
        return me - 1 + 2 * side

    def peer(stage, j):
        size, stride = stages[stage]
        digit = lax.rem(chip // stride, size)
        return digit, (chip + (lax.rem(digit + j, size) - digit) * stride) * 2 + 1

    barrier = pltpu.get_barrier_semaphore()

    def greet(other):
        pl.semaphore_signal(barrier, inc=1, device_id=(other,), device_id_type=MESH)

    for side in range(2):
        @pl.when(present(side))
        def _():
            greet(neighbour(side))

    @pl.when(odd == 1)
    def _():
        for stage, (size, _) in enumerate(stages):
            for j in range(1, size):
                greet(peer(stage, j)[1])

    for plane in range(depth):
        for which in range(2):
            load(plane, which).start()

    blank = jnp.zeros((PAD, cols), jnp.float32)
    for ref in (u0, u1, solid):
        for plane in range(ref.shape[0]):
            ref[plane, 0:PAD, :] = blank
            ref[plane, rows + PAD:rows + 2 * PAD, :] = blank
    for side in range(2):
        @pl.when(jnp.logical_not(present(side)))
        def _():
            bits_in[side] = jnp.zeros((2, words, cols), jnp.int32)

            def clear(t, carry):
                at = pl.ds(pl.multiple_of(t * TILE, TILE), TILE)
                halo_r[side, at, :] = jnp.zeros((TILE, cols), jnp.float32)
                halo_u[side, at, :] = jnp.zeros((TILE, cols), jnp.float32)
                return carry

            lax.fori_loop(0, rows // TILE, clear, 0)

    def halo_copy(phase, side, k):
        at = pl.multiple_of(k * chunk, chunk)
        plane = side * (depth - 1)
        if phase == 0:
            source, target = r0.at[plane, pl.ds(at, chunk)], halo_r
        else:
            source, target = u1.at[plane, pl.ds(pl.multiple_of(at + PAD, PAD), chunk)], halo_u
        return pltpu.make_async_remote_copy(
            src_ref=source,
            dst_ref=target.at[1 - side, pl.ds(at, chunk)],
            send_sem=halo_send.at[phase, side, k],
            recv_sem=halo_recv.at[phase, 1 - side, k],
            device_id=(neighbour(side),),
            device_id_type=MESH,
        )

    def halo_arrival(phase, side, k):
        at = pl.multiple_of(k * chunk, chunk)
        target = halo_r if phase == 0 else halo_u
        return pltpu.make_async_remote_copy(
            src_ref=target.at[side, pl.ds(at, chunk)],
            dst_ref=target.at[side, pl.ds(at, chunk)],
            send_sem=halo_send.at[phase, side, k],
            recv_sem=halo_recv.at[phase, side, k],
            device_id=(neighbour(side),),
            device_id_type=MESH,
        )

    def send_halo(phase, side, k):
        @pl.when(present(side))
        def _():
            halo_copy(phase, side, k).start()

    def send_plane(phase, side):
        def one(k, carry):
            send_halo(phase, side, k)
            return carry

        lax.fori_loop(0, chunks, one, 0)

    def wait_halo(phase, side, k):
        @pl.when(present(side))
        def _():
            halo_arrival(phase, side, k).wait_recv()

    def row(k, t):
        return pl.multiple_of(k * chunk + t * TILE, TILE)

    outer = sorted({0, 1, depth - 2, depth - 1})
    steps = rows // TILE
    for plane in range(depth):
        load(plane, 0).wait()
        load(plane, 1).wait()

        def mask_tile(t, carry, plane=plane):
            at = pl.ds(pl.multiple_of(t * TILE, TILE), TILE)
            r0[plane, at, :] = jnp.where(flags[plane, at, :] == 1, rhs[plane, at, :], 0.0)
            return carry

        lax.fori_loop(0, steps, mask_tile, 0)

        def pack(j, word, plane=plane):
            at = pl.ds(pl.multiple_of(j * words, words), words)
            is_solid = flags[plane, at, :] == 2
            padded = pl.ds(pl.multiple_of(j * words + PAD, PAD), words)
            solid[plane + 2, padded, :] = jnp.where(is_solid, 1.0, 0.0)
            return word | jnp.left_shift(jnp.where(is_solid, 1, 0), j)

        word = lax.fori_loop(0, 32, pack, jnp.zeros((words, cols), jnp.int32))
        if plane in outer:
            bits_out[outer.index(plane)] = word

    def bit_copy(side):
        lead = 0 if side == 0 else len(outer) - 2
        return pltpu.make_async_remote_copy(
            src_ref=bits_out.at[pl.ds(lead, 2)],
            dst_ref=bits_in.at[1 - side],
            send_sem=bit_send.at[side],
            recv_sem=bit_recv.at[1 - side],
            device_id=(neighbour(side),),
            device_id_type=MESH,
        )

    greeted = sum(size - 1 for size, _ in stages)
    callers = present(0).astype(jnp.int32) + present(1).astype(jnp.int32) + odd * greeted
    pl.semaphore_wait(barrier, callers)

    for side in range(2):
        @pl.when(present(side))
        def _():
            bit_copy(side).start()
    send_plane(0, far_side)
    send_plane(0, near_side)

    for side in range(2):
        @pl.when(present(side))
        def _():
            bit_copy(1 - side).wait_recv()
        for i in range(2):
            def unpack(j, carry, side=side, i=i):
                padded = pl.ds(pl.multiple_of(j * words + PAD, PAD), words)
                bit = jnp.bitwise_and(jnp.right_shift(bits_in[side, i], j), 1)
                solid[side * (depth + 2) + i, padded, :] = bit.astype(jnp.float32)
                return carry

            lax.fori_loop(0, 32, unpack, 0)

    column = lax.broadcasted_iota(jnp.int32, (TILE, cols), 1)

    def inplane(ref, plane, start):
        block = ref[plane, pl.ds(start, TILE + 2 * PAD), :]
        centre = block[PAD:PAD + TILE]
        total = block[PAD - 1:PAD - 1 + TILE] + block[PAD + 1:PAD + 1 + TILE]
        total = total + jnp.where(column == 0, 0.0, pltpu.roll(centre, 1, 1))
        total = total + jnp.where(column == cols - 1, 0.0, pltpu.roll(centre, cols - 1, 1))
        return centre, total

    def centre_of(ref, plane, start):
        return ref[plane, pl.ds(pl.multiple_of(start + PAD, PAD), TILE), :]

    def put(ref, plane, start, value):
        ref[plane, pl.ds(pl.multiple_of(start + PAD, PAD), TILE), :] = value

    def fold(value):
        total = value[0:8]
        for i in range(8, TILE, 8):
            total = total + value[i:i + 8]
        return total

    none = jnp.zeros((8, cols), jnp.float32)

    def inverse(plane, start):
        _, total = inplane(solid, plane + 1, start)
        total = total + centre_of(solid, plane, start) + centre_of(solid, plane + 2, start)
        return 1.0 / jnp.maximum(6.0 - total, 1.0)

    def first(t, moment):
        start = pl.multiple_of(t * TILE, TILE)
        at = pl.ds(start, TILE)
        for plane in range(depth):
            value = jnp.where(flags[plane, at, :] == 1, inverse(plane + 1, start), 0.0)
            inv[plane + 1, at, :] = value
            residual = r0[plane, at, :]
            precond = residual * value
            put(u0, plane, start, precond)
            moment = moment + fold(residual * precond)
        for plane in (0, depth + 1):
            inv[plane, at, :] = inverse(plane, start)
        return moment

    moment0 = lax.fori_loop(0, steps, first, none)

    def local_part(field, scaled, out, plane, start):
        at = pl.ds(start, TILE)
        _, total = inplane(field, plane, start)
        if plane > 0:
            total = total + centre_of(field, plane - 1, start)
        if plane < depth - 1:
            total = total + centre_of(field, plane + 1, start)
        image = jnp.where(inv[plane + 1, at, :] > 0.0, scaled[plane, at, :] - total, 0.0)
        out[plane, at, :] = image
        return image

    def apply_once(plane, start, image, value, moments):
        precond = image * value
        put(u1, plane, start, precond)
        return (
            moments[0] + fold(image * centre_of(u0, plane, start)),
            moments[1] + fold(image * precond),
        )

    def second(t, moments):
        start = pl.multiple_of(t * TILE, TILE)
        for plane in range(depth):
            image = local_part(u0, r0, w0, plane, start)
            if 0 < plane < depth - 1:
                value = inv[plane + 1, pl.ds(start, TILE), :]
                moments = apply_once(plane, start, image, value, moments)
        return moments

    moments = lax.fori_loop(0, steps, second, (none, none))

    def edge_one(side, moments, forward):
        plane = side * (depth - 1)

        def step(k, moments):
            wait_halo(0, side, k)

            def tile(t, moments):
                start = row(k, t)
                at = pl.ds(start, TILE)
                value = inv[plane + 1, at, :]
                beyond = halo_r[side, at, :] * inv[side * (depth + 1), at, :]
                image = jnp.where(value > 0.0, w0[plane, at, :] - beyond, 0.0)
                w0[plane, at, :] = image
                return apply_once(plane, start, image, value, moments)

            moments = lax.fori_loop(0, tiles, tile, moments)

            @pl.when(forward)
            def _():
                send_halo(1, side, k)

            return moments

        return lax.fori_loop(0, chunks, step, moments)

    moments = edge_one(near_side, moments, odd >= 0)
    moment1, moment2 = edge_one(far_side, moments, odd == 1)

    def third(t, moment):
        start = pl.multiple_of(t * TILE, TILE)
        for plane in range(depth):
            image = local_part(u1, w0, w1, plane, start)
            moment = moment + fold(image * centre_of(u1, plane, start))
        return moment

    moment3 = lax.fori_loop(0, steps, third, none)

    def edge_two(side, moment, weight, after):
        plane = side * (depth - 1)

        def step(k, moment):
            wait_halo(1, side, k)
            after(k)

            def tile(t, moment):
                start = row(k, t)
                at = pl.ds(start, TILE)
                beyond = halo_u[side, at, :]
                image = jnp.where(inv[plane + 1, at, :] > 0.0, w1[plane, at, :] - beyond, 0.0)
                w1[plane, at, :] = image
                return moment - weight * fold(beyond * centre_of(u1, plane, start))

            return lax.fori_loop(0, tiles, tile, moment)

        return lax.fori_loop(0, chunks, step, moment)

    def lanes(value):
        total = value[:, 0:128]
        for i in range(128, cols, 128):
            total = total + value[:, i:i + 128]
        return jnp.sum(total, axis=0, keepdims=True)

    def settle(moment):
        pair[0, 0:1, :] = lanes(moment0)
        pair[0, 1:2, :] = lanes(moment1)
        pair[0, 2:3, :] = lanes(moment2)
        pair[0, 3:4, :] = lanes(moment)
        pair[0, 4:8, :] = jnp.zeros((4, 128), jnp.float32)

    moment3 = edge_two(near_side, moment3, 1.0, lambda k: None)

    def pair_copy():
        return pltpu.make_async_remote_copy(
            src_ref=pair.at[0], dst_ref=pair.at[1], send_sem=pair_send, recv_sem=pair_recv,
            device_id=(partner,), device_id_type=MESH,
        )

    def total_copy():
        return pltpu.make_async_remote_copy(
            src_ref=totals, dst_ref=totals, send_sem=total_send, recv_sem=total_recv,
            device_id=(partner,), device_id_type=MESH,
        )

    def sum_copy(stage, j):
        digit, other = peer(stage, j)
        return pltpu.make_async_remote_copy(
            src_ref=mine.at[stage],
            dst_ref=got.at[stage, digit],
            send_sem=sum_send.at[stage, j],
            recv_sem=sum_recv.at[stage, digit],
            device_id=(other,),
            device_id_type=MESH,
        )

    def sum_arrival(stage, j):
        digit, other = peer(stage, j)
        slot = lax.rem(digit + j, stages[stage][0])
        return pltpu.make_async_remote_copy(
            src_ref=got.at[stage, slot],
            dst_ref=got.at[stage, slot],
            send_sem=sum_send.at[stage, j],
            recv_sem=sum_recv.at[stage, slot],
            device_id=(other,),
            device_id_type=MESH,
        )

    @pl.when(odd == 0)
    def _():
        def send_late(k):
            @pl.when(k == max(chunks - 2, 0))
            def _():
                send_plane(1, 0)

        settle(edge_two(0, moment3, 2.0, send_late))
        pair_copy().start()
        total_copy().wait_recv()

    @pl.when(odd == 1)
    def _():
        settle(moment3)
        pair_copy().wait_recv()
        total = pair[0] + pair[1]
        for stage, (size, _) in enumerate(stages):
            mine[stage] = total
            for j in range(1, size):
                sum_copy(stage, j).start()
            got[stage, peer(stage, 0)[0]] = total
            for j in range(1, size):
                sum_arrival(stage, j).wait_recv()
            total = got[stage, 0]
            for i in range(1, size):
                total = total + got[stage, i]
        totals[...] = total
        total_copy().start()

    everyone = totals[...]
    s0, s1, s2, s3 = (everyone[i:i + 1] for i in range(4))

    def whole(value):
        return jnp.sum(value, axis=1, keepdims=True)

    rz_old = whole(s0)
    step_old = rz_old / whole(s1)
    rz_now = whole(s0 - 2.0 * step_old * s1 + step_old * step_old * s2)
    grown = 1.0 + rz_now / rz_old
    product = whole(grown * grown * s1 - 2.0 * step_old * grown * s2 + step_old * step_old * s3)
    step_size = rz_now / product
    lead = step_old + step_size * grown
    trail = step_size * step_old

    for plane in range(depth):
        def last(t, carry, plane=plane):
            start = pl.multiple_of(t * TILE, TILE)
            at = pl.ds(start, TILE)
            base = r0[plane, at, :]
            along = w0[plane, at, :]
            sol_ref[plane, at, :] = inv[plane + 1, at, :] * (lead * base - trail * along)
            res_ref[plane, at, :] = base - lead * along + trail * w1[plane, at, :]
            return carry

        lax.fori_loop(0, steps, last, 0)

    @pl.when(jnp.logical_and(odd == 1, present(1)))
    def _():
        plane = depth - 1

        def late(k, carry):
            halo_arrival(1, 1, k).wait_recv()

            def tile(t, carry):
                at = pl.ds(row(k, t), TILE)
                beyond = jnp.where(inv[plane + 1, at, :] > 0.0, halo_u[1, at, :], 0.0)
                res_ref[plane, at, :] = res_ref[plane, at, :] - trail * beyond
                return carry

            return lax.fori_loop(0, tiles, tile, carry)

        lax.fori_loop(0, chunks, late, 0)

    for side in range(2):
        @pl.when(present(side))
        def _():
            bit_copy(side).wait_send()
            for phase in range(2):
                for k in range(chunks):
                    halo_copy(phase, side, k).wait_send()

    @pl.when(odd == 0)
    def _():
        pair_copy().wait_send()

    @pl.when(odd == 1)
    def _():
        total_copy().wait_send()
        for stage, (size, _) in enumerate(stages):
            for j in range(1, size):
                sum_copy(stage, j).wait_send()


def groups(chips):
    size = math.gcd(chips, 4)
    stages, stride = [(size, 1)], size
    while stride < chips:
        rest = chips // stride
        size = 2 if rest % 2 == 0 else rest
        stages.append((size, stride))
        stride *= size
    return stages


def body(count, right_side, cell_flags):
    depth, rows, cols = right_side.shape
    stages = groups(count // 2)
    widest = max(size for size, _ in stages)
    chunk = math.gcd(rows, 64)
    chunks = rows // chunk
    f32 = jnp.float32
    field = pltpu.VMEM((depth, rows, cols), f32)
    padded = pltpu.VMEM((depth, rows + 2 * PAD, cols), f32)
    outer = len({0, 1, depth - 2, depth - 1})
    dma = pltpu.SemaphoreType.DMA
    grant = VMEM_BYTES - 8 * right_side.size - 2**19
    return pl.pallas_call(
        functools.partial(kernel, count, chunk, stages),
        out_shape=(field, field),
        in_specs=[pl.BlockSpec(memory_space=pltpu.HBM)] * 2,
        out_specs=(pl.BlockSpec(memory_space=pltpu.VMEM),) * 2,
        scratch_shapes=[
            field,
            pltpu.VMEM((depth, rows, cols), jnp.int32),
            field,
            pltpu.VMEM((depth + 2, rows, cols), f32),
            pltpu.VMEM((depth + 4, rows + 2 * PAD, cols), f32),
            padded, padded, field, field,
            pltpu.VMEM((2, rows, cols), f32),
            pltpu.VMEM((2, rows, cols), f32),
            pltpu.VMEM((outer, rows // 32, cols), jnp.int32),
            pltpu.VMEM((2, 2, rows // 32, cols), jnp.int32),
            pltpu.VMEM((2, 8, 128), f32),
            pltpu.VMEM((8, 128), f32),
            pltpu.VMEM((len(stages), 8, 128), f32),
            pltpu.VMEM((len(stages), widest, 8, 128), f32),
            dma((2, depth)),
            dma((2,)), dma((2,)),
            dma((2, 2, chunks)), dma((2, 2, chunks)),
            dma, dma, dma, dma,
            dma((len(stages), widest)), dma((len(stages), widest)),
        ],
        compiler_params=pltpu.CompilerParams(
            collective_id=0, has_side_effects=True, vmem_limit_bytes=grant
        ),
    )(right_side, cell_flags)


def solution(mesh):
    placed = (P("gz", None, None), P("gz", None, None))
    return jax.shard_map(
        functools.partial(body, mesh.shape["gz"]),
        mesh=mesh,
        in_specs=placed,
        out_specs=placed,
        check_vma=False,
    )
```

time: 67.5 us -> 68.1 us (level); the launches traced: 66.2 us -> 68 us
  Pallas kernels: 62.9 us -> 64.7 us
    pallas_call x1, Pallas kernels: 62.9 us -> 64.7 us  [body(): pl.pallas_call(functools.partial(kernel, count, chunk, stages), out_shape...]
where the time goes in v1:
time: 68.1 us; the launch traced here: 68 us
  Pallas kernels  64.7 us (95%)
  local copies, waits for them, and re-layouts  2.64 us (4%)
    pallas_call x1, Pallas kernels, body(): pl.pallas_call(functools.partial(kernel, count, chunk, stages), out_shape...  64.7 us
    unnamed x2, local copies, waits for them, and re-layouts  2.64 us

profile of v1, /device:TPU:1, one launch (start us, length us, event | category | flops | bytes accessed | tf_op | source)
XLA Modules:
  0.0 68.0 jit_solution(14760813084446311394)
XLA Ops:
  0.6 64.7 %shard_map.41 = (f32[2,512,512]{2,1,0:T(8,128)S(1)}, f32[2,512,512]{2,1,0:T(8,128)S(1)}) custom-call(f32[2,512,512]{2,1,0:T(8,128)} %side_hbm.1, s32[2,512,512]{2,1,0:T(8,128)} %flag_hbm.1), custom_call_target="tpu_custom_call" | custom-call | tf_op jit(solution)/shard_map/pallas_call | solution.py:491
  65.3 1.3 %copy.6 = f32[2,512,512]{2,1,0:T(8,128)} copy(f32[2,512,512]{2,1,0:T(8,128)S(1)} %get-tuple-element.2) | data formatting | bytes 4194304
  66.7 1.3 %copy.7 = f32[2,512,512]{2,1,0:T(8,128)} copy(f32[2,512,512]{2,1,0:T(8,128)S(1)} %get-tuple-element.3) | data formatting | bytes 4194304

commit v2 on v1

--- a/solution.py
+++ b/solution.py
@@ -175,7 +175,10 @@
         @pl.when(present(side))
         def _():
             bit_copy(side).start()
-    send_plane(0, far_side)
+    @pl.when(odd == 0)
+    def _():
+        send_plane(0, 0)
+
     send_plane(0, near_side)
 
     for side in range(2):
@@ -266,6 +269,10 @@
 
     moments = lax.fori_loop(0, steps, second, (none, none))
 
+    @pl.when(odd == 1)
+    def _():
+        send_plane(0, 1)
+
     def edge_one(side, moments, forward):
         plane = side * (depth - 1)
 
@@ -329,17 +336,15 @@
         return jnp.sum(total, axis=0, keepdims=True)
 
     def settle(moment):
-        pair[0, 0:1, :] = lanes(moment0)
-        pair[0, 1:2, :] = lanes(moment1)
-        pair[0, 2:3, :] = lanes(moment2)
-        pair[0, 3:4, :] = lanes(moment)
-        pair[0, 4:8, :] = jnp.zeros((4, 128), jnp.float32)
+        for i, value in enumerate((moment0, moment1, moment2, moment)):
+            mine[0, i:i + 1, :] = lanes(value)
+        mine[0, 4:8, :] = jnp.zeros((4, 128), jnp.float32)
 
     moment3 = edge_two(near_side, moment3, 1.0, lambda k: None)
 
     def pair_copy():
         return pltpu.make_async_remote_copy(
-            src_ref=pair.at[0], dst_ref=pair.at[1], send_sem=pair_send, recv_sem=pair_recv,
+            src_ref=mine.at[0], dst_ref=pair, send_sem=pair_send, recv_sem=pair_recv,
             device_id=(partner,), device_id_type=MESH,
         )
 
@@ -360,41 +365,63 @@
             device_id_type=MESH,
         )
 
-    def sum_arrival(stage, j):
-        digit, other = peer(stage, j)
-        slot = lax.rem(digit + j, stages[stage][0])
+    def sum_arrival(stage, slot):
         return pltpu.make_async_remote_copy(
             src_ref=got.at[stage, slot],
             dst_ref=got.at[stage, slot],
-            send_sem=sum_send.at[stage, j],
+            send_sem=sum_send.at[stage, 0],
             recv_sem=sum_recv.at[stage, slot],
-            device_id=(other,),
+            device_id=(partner,),
             device_id_type=MESH,
         )
 
+    near_size = stages[0][0]
+    ahead = min(2, chunks)
+
     @pl.when(odd == 0)
     def _():
-        def send_late(k):
-            @pl.when(k == max(chunks - 2, 0))
+        def early(k):
+            @pl.when(k == max(chunks - 3, 0))
             def _():
-                send_plane(1, 0)
-
-        settle(edge_two(0, moment3, 2.0, send_late))
+                for i in range(ahead):
+                    send_halo(1, 0, i)
+
+        settle(edge_two(0, moment3, 2.0, early))
+        pair_copy().wait_recv()
+        mine[0] = mine[0] + pair[...]
+        for j in range(near_size):
+            sum_copy(0, j).start()
+
+        @pl.when(present(0))
+        def _():
+            def pace(k, carry):
+                halo_copy(1, 0, k - ahead).wait_send()
+                halo_copy(1, 0, k).start()
+                return carry
+
+            lax.fori_loop(ahead, chunks, pace, 0)
+
+        total_copy().wait_recv()
+
+    @pl.when(odd == 1)
+    def _():
+        settle(moment3)
         pair_copy().start()
-        total_copy().wait_recv()
-
-    @pl.when(odd == 1)
-    def _():
-        settle(moment3)
-        pair_copy().wait_recv()
-        total = pair[0] + pair[1]
+        for i in range(near_size):
+            sum_arrival(0, i).wait_recv()
+        total = got[0, 0]
+        for i in range(1, near_size):
+            total = total + got[0, i]
         for stage, (size, _) in enumerate(stages):
+            if stage == 0:
+                continue
             mine[stage] = total
             for j in range(1, size):
                 sum_copy(stage, j).start()
-            got[stage, peer(stage, 0)[0]] = total
+            digit = peer(stage, 0)[0]
+            got[stage, digit] = total
             for j in range(1, size):
-                sum_arrival(stage, j).wait_recv()
+                sum_arrival(stage, lax.rem(digit + j, size)).wait_recv()
             total = got[stage, 0]
             for i in range(1, size):
                 total = total + got[stage, i]
@@ -451,16 +478,25 @@
             bit_copy(side).wait_send()
             for phase in range(2):
                 for k in range(chunks):
-                    halo_copy(phase, side, k).wait_send()
+                    if phase == 1 and side == 0 and k < chunks - min(2, chunks):
+                        @pl.when(odd == 1)
+                        def _():
+                            halo_copy(phase, side, k).wait_send()
+                    else:
+                        halo_copy(phase, side, k).wait_send()
 
     @pl.when(odd == 0)
     def _():
+        for j in range(near_size):
+            sum_copy(0, j).wait_send()
+
+    @pl.when(odd == 1)
+    def _():
         pair_copy().wait_send()
-
-    @pl.when(odd == 1)
-    def _():
         total_copy().wait_send()
         for stage, (size, _) in enumerate(stages):
+            if stage == 0:
+                continue
             for j in range(1, size):
                 sum_copy(stage, j).wait_send()
 
@@ -504,7 +540,7 @@
             pltpu.VMEM((2, rows, cols), f32),
             pltpu.VMEM((outer, rows // 32, cols), jnp.int32),
             pltpu.VMEM((2, 2, rows // 32, cols), jnp.int32),
-            pltpu.VMEM((2, 8, 128), f32),
+            pltpu.VMEM((8, 128), f32),
             pltpu.VMEM((8, 128), f32),
             pltpu.VMEM((len(stages), 8, 128), f32),
             pltpu.VMEM((len(stages), widest, 8, 128), f32),

time: 68.1 us -> 59.1 us (0.87); the launches traced: 68 us -> 58.2 us
  Pallas kernels: 64.7 us -> 54.9 us
    pallas_call x1, Pallas kernels: 64.7 us -> 54.9 us  [body(): pl.pallas_call(functools.partial(kernel, count, chunk, stages), out_shape...]
where the time goes in v2:
time: 59.1 us; the launch traced here: 58.2 us
  Pallas kernels  54.9 us (93%)
  local copies, waits for them, and re-layouts  2.64 us (4%)
  between operations  0.64 us (1%)
    pallas_call x1, Pallas kernels, body(): pl.pallas_call(functools.partial(kernel, count, chunk, stages), out_shape...  54.9 us
    unnamed x2, local copies, waits for them, and re-layouts  2.64 us

profile of v2, /device:TPU:1, one launch (start us, length us, event | category | flops | bytes accessed | tf_op | source)
XLA Modules:
  0.0 58.2 jit_solution(11124851491512310401)
XLA Ops:
  0.6 54.9 %shard_map.41 = (f32[2,512,512]{2,1,0:T(8,128)S(1)}, f32[2,512,512]{2,1,0:T(8,128)S(1)}) custom-call(f32[2,512,512]{2,1,0:T(8,128)} %side_hbm.1, s32[2,512,512]{2,1,0:T(8,128)} %flag_hbm.1), custom_call_target="tpu_custom_call" | custom-call | tf_op jit(solution)/shard_map/pallas_call | solution.py:527
  55.5 1.3 %copy.6 = f32[2,512,512]{2,1,0:T(8,128)} copy(f32[2,512,512]{2,1,0:T(8,128)S(1)} %get-tuple-element.2) | data formatting | bytes 4194304
  56.8 1.3 %copy.7 = f32[2,512,512]{2,1,0:T(8,128)} copy(f32[2,512,512]{2,1,0:T(8,128)S(1)} %get-tuple-element.3) | data formatting | bytes 4194304

commit v3 on v2

v3 whole, which is shorter than its diff:
```python
import functools
import math

import jax
import jax.numpy as jnp
from jax import lax
from jax.experimental import pallas as pl
from jax.experimental.pallas import tpu as pltpu
from jax.sharding import PartitionSpec as P

MESH = pl.DeviceIdType.MESH
TILE = 16
LAST = 64
CHUNK = 64
AFTER = 128
LAGS = (192, 256)
BURSTS = (128, 192)
HOLDS = (64, 192)
WINDOW = 256
PAD = 8
VMEM_BYTES = 67_043_328


def kernel(
    count, chunk, stages,
    side_hbm, flag_hbm, sol_ref, res_ref,
    rhs, flags, r0, inv, shadow, u0, u1, w0, w1, halo_r, halo_u, solid, fluid, code,
    pair, mine, got,
    in_sem, go, known, bit_send, bit_recv, halo_send, halo_recv,
    pair_send, pair_recv, sum_send, sum_recv,
):
    depth, rows, cols = rhs.shape
    words = rows // 32
    chunks = rows // chunk
    tiles = chunk // TILE
    steps = rows // TILE

    def pieces(length):
        return min(max(length // chunk, 1), chunks)

    deep = pieces(WINDOW)
    final = math.gcd(rows, LAST)
    near_size, far_size = stages[0][0], stages[1][0]
    me = lax.axis_index("gz")
    chip, odd = me // 2, lax.rem(me, 2)
    is_even, is_odd = odd == 0, odd == 1
    near_side, far_side = 1 - odd, odd
    near_plane, far_plane = near_side * (depth - 1), far_side * (depth - 1)
    partner = me + 1 - 2 * odd
    has_far = jnp.where(is_even, me > 0, me < count - 1)

    digit = lax.rem(chip, near_size)
    relief = near_size // 2 if near_size > 2 else 0
    is_first, is_relief = digit == 0, digit == relief

    def by_place(lengths):
        return jnp.where(is_first, pieces(lengths[1]), pieces(lengths[0]))

    lag, burst, hold = by_place(LAGS), by_place(BURSTS), by_place(HOLDS)

    def load(plane, which):
        source, target = ((flag_hbm, flags), (side_hbm, rhs))[which]
        return pltpu.make_async_copy(source.at[plane], target.at[plane], in_sem.at[which, plane])

    def peer(stage, j):
        size, stride = stages[stage]
        digit = lax.rem(chip // stride, size)
        return digit, chip + (lax.rem(digit + j, size) - digit) * stride

    barrier = pltpu.get_barrier_semaphore()

    def greet(other):
        pl.semaphore_signal(barrier, inc=1, device_id=(other,), device_id_type=MESH)

    @pl.when(has_far)
    def _():
        greet(me - 1 + 2 * odd)

    greet(partner)
    inner_planes = list(range(1, depth - 1))
    load(far_plane, 0).start()
    for plane in [near_plane] + inner_planes:
        load(plane, 0).start()
    load(far_plane, 1).start()
    for plane in [near_plane] + inner_planes:
        load(plane, 1).start()
    pairs = far_size & (far_size - 1) == 0
    if pairs:
        rounds = [(far_size >> i,) for i in range(1, far_size.bit_length())]
    else:
        rounds = [tuple(range(1, far_size))]

    def far_peer(distance):
        digit = chip // near_size
        if pairs:
            step = distance * (1 - 2 * lax.rem(digit // distance, 2))
        else:
            step = lax.rem(digit + distance, far_size) - digit
        return 2 * (chip + step * near_size) + 1

    if relief:
        @pl.when(is_even)
        def _():
            greet(2 * (chip - digit + lax.rem(digit + relief, near_size)) + 1)

    @pl.when(is_odd)
    def _():
        for group in rounds:
            for distance in group:
                greet(far_peer(distance))
        for j in range(1, near_size):
            greet(2 * peer(0, j)[1] + 1)

    def tell(which):
        for distance in rounds[which]:
            pl.semaphore_signal(
                known.at[which], inc=1, device_id=(far_peer(distance),), device_id_type=MESH
            )

    def hear(which):
        pl.semaphore_wait(known.at[which], len(rounds[which]))
        if which + 1 < len(rounds):
            tell(which + 1)

    blank = jnp.zeros((PAD, cols), jnp.float32)
    for ref in (u0, u1):
        for plane in range(ref.shape[0]):
            ref[plane, 0:PAD, :] = blank
            ref[plane, rows + PAD:rows + 2 * PAD, :] = blank

    @pl.when(jnp.logical_not(has_far))
    def _():
        solid[far_side * (depth + 2)] = jnp.zeros((words, cols), jnp.int32)
        solid[far_side * (depth + 2) + 1] = jnp.zeros((words, cols), jnp.int32)

        def clear(t, carry):
            at = pl.ds(pl.multiple_of(t * TILE, TILE), TILE)
            halo_r[far_side, at, :] = jnp.zeros((TILE, cols), jnp.float32)
            halo_u[far_side, at, :] = jnp.zeros((TILE, cols), jnp.float32)
            return carry

        lax.fori_loop(0, steps, clear, 0)

    def on(side, there):
        if side is far_side:
            pl.when(has_far)(there)
        else:
            there()

    def halo_copy(phase, side, k, raw=False):
        at = pl.multiple_of(k * chunk, chunk)
        plane = side * (depth - 1)
        if raw:
            source = r0.at[plane, pl.ds(at, chunk)]
        else:
            field = (u0, u1)[phase]
            source = field.at[plane, pl.ds(pl.multiple_of(at + PAD, PAD), chunk)]
        return pltpu.make_async_remote_copy(
            src_ref=source,
            dst_ref=(halo_r, halo_u)[phase].at[1 - side, pl.ds(at, chunk)],
            send_sem=halo_send.at[phase, side, k],
            recv_sem=halo_recv.at[phase, 1 - side, k],
            device_id=(me - 1 + 2 * side,),
            device_id_type=MESH,
        )

    def halo_arrival(phase, side, k):
        at = pl.multiple_of(k * chunk, chunk)
        target = (halo_r, halo_u)[phase].at[side, pl.ds(at, chunk)]
        return pltpu.make_async_remote_copy(
            src_ref=target,
            dst_ref=target,
            send_sem=halo_send.at[phase, side, k],
            recv_sem=halo_recv.at[phase, side, k],
            device_id=(me - 1 + 2 * side,),
            device_id_type=MESH,
        )

    def wait_halo(phase, side, k):
        on(side, lambda: halo_arrival(phase, side, k).wait_recv())

    def send_plane(phase, side, first=0, raw=False, last=chunks):
        def all_chunks():
            def one(k, carry):
                halo_copy(phase, side, k, raw).start()
                return carry

            lax.fori_loop(first, last, one, 0)

        on(side, all_chunks)

    def sent_plane(phase, side, first=0, last=chunks):
        def all_chunks():
            def one(k, carry):
                halo_copy(phase, side, k).wait_send()
                return carry

            lax.fori_loop(first, last, one, 0)

        on(side, all_chunks)

    def bit_copy(side, planes, arrival=False):
        mine_at, theirs_at = 2 + side * (depth - 1), 1 + (1 - side) * (depth + 1)
        halo_at = 1 + side * (depth + 1)
        return pltpu.make_async_remote_copy(
            src_ref=solid.at[pl.ds(halo_at if arrival else mine_at, planes)],
            dst_ref=solid.at[pl.ds(halo_at if arrival else theirs_at, planes)],
            send_sem=bit_send.at[side],
            recv_sem=bit_recv.at[side if arrival else 1 - side],
            device_id=(me - 1 + 2 * side,),
            device_id_type=MESH,
        )

    def row(k, t):
        return pl.multiple_of(k * chunk + t * TILE, TILE)

    def mask(plane, first, last):
        def tile(t, carry):
            at = pl.ds(pl.multiple_of(t * TILE, TILE), TILE)
            r0[plane, at, :] = jnp.where(flags[plane, at, :] == 1, rhs[plane, at, :], 0.0)
            return carry

        lax.fori_loop(first, last, tile, 0)

    def pack(plane):
        def one(j, found):
            at = pl.ds(pl.multiple_of(j * words, words), words)
            kinds = flags[plane, at, :]
            return tuple(
                word | jnp.left_shift(jnp.where(kinds == kind, 1, 0), j)
                for word, kind in zip(found, (2, 1))
            )

        empty = jnp.zeros((words, cols), jnp.int32)
        solid[plane + 2], fluid[plane] = lax.fori_loop(0, 32, one, (empty, empty))

    for plane in [far_plane, near_plane] + inner_planes:
        load(plane, 0).wait()
        pack(plane)
    greeted = sum(len(group) for group in rounds) + near_size - 1 + (relief > 0)
    pl.semaphore_wait(barrier, 1 + has_far.astype(jnp.int32) + odd * greeted)

    @pl.when(is_even)
    def _():
        on(far_side, lambda: bit_copy(0, 2).start())

    @pl.when(is_odd)
    def _():
        on(far_side, lambda: bit_copy(1, 1).start())
        if rounds:
            tell(0)

    bit_copy(near_side, 1).start()
    load(far_plane, 1).wait()
    mask(far_plane, 0, steps)

    @pl.when(is_even)
    def _():
        send_plane(0, far_side, 0, True)

    for plane in [near_plane] + inner_planes:
        load(plane, 1).wait()
        mask(plane, 0, steps)

    bit_copy(near_side, 1, True).wait_recv()

    @pl.when(is_even)
    def _():
        on(far_side, lambda: bit_copy(0, 1, True).wait_recv())

    @pl.when(is_odd)
    def _():
        on(far_side, lambda: bit_copy(1, 2, True).wait_recv())

    def classify(at, slot, known_fluid):
        word = solid[at]
        line = lax.broadcasted_iota(jnp.int32, (words, cols), 0)
        across = lax.broadcasted_iota(jnp.int32, (words, cols), 1)
        before, after = pltpu.roll(word, 1, 0), pltpu.roll(word, words - 1, 0)
        before = jnp.where(line == 0, jnp.left_shift(before, 1), before)
        after = jnp.where(line == words - 1, lax.shift_right_logical(after, 1), after)
        left = jnp.where(across == 0, 0, pltpu.roll(word, 1, 1))
        right = jnp.where(across == cols - 1, 0, pltpu.roll(word, cols - 1, 1))

        def add(a, b, c):
            return a ^ b ^ c, (a & b) | (c & (a ^ b))

        ones, twos = add(before, after, left)
        more_ones, more_twos = add(right, solid[at - 1], solid[at + 1])
        digits = [ones ^ more_ones, *add(twos, more_twos, ones & more_ones)]
        for i, digit in enumerate(digits):
            if known_fluid is not None:
                digit = digit | ~known_fluid
            code[slot, i] = digit

    def inverse(slot, j):
        bit = jnp.left_shift(1, j)
        ones, twos, fours = ((code[slot, i] & bit) != 0 for i in range(3))
        none, one, two, three, four, five, six, out = (
            jnp.float32(value) for value in (1 / 6, 1 / 5, 1 / 4, 1 / 3, 1 / 2, 1.0, 1.0, 0.0)
        )
        low = jnp.where(twos, jnp.where(ones, three, two), jnp.where(ones, one, none))
        high = jnp.where(twos, jnp.where(ones, out, six), jnp.where(ones, five, four))
        return jnp.where(fours, high, low)

    column = lax.broadcasted_iota(jnp.int32, (TILE, cols), 1)

    def inplane(ref, plane, start):
        block = ref[plane, pl.ds(start, TILE + 2 * PAD), :]
        centre = block[PAD:PAD + TILE]
        total = block[PAD - 1:PAD - 1 + TILE] + block[PAD + 1:PAD + 1 + TILE]
        total = total + jnp.where(column == 0, 0.0, pltpu.roll(centre, 1, 1))
        total = total + jnp.where(column == cols - 1, 0.0, pltpu.roll(centre, cols - 1, 1))
        return centre, total

    def centre_of(ref, plane, start):
        return ref[plane, pl.ds(pl.multiple_of(start + PAD, PAD), TILE), :]

    def put(ref, plane, start, value):
        ref[plane, pl.ds(pl.multiple_of(start + PAD, PAD), TILE), :] = value

    def fold(value):
        total = value[0:8]
        for i in range(8, value.shape[0], 8):
            total = total + value[i:i + 8]
        return total

    none = jnp.zeros((8, cols), jnp.float32)

    for plane in range(depth):
        classify(plane + 2, plane, fluid[plane])

    def first(j, moment):
        start = pl.multiple_of(j * words, words)
        at = pl.ds(start, words)
        padded = pl.ds(pl.multiple_of(start + PAD, PAD), words)
        for plane in range(depth):
            value = inverse(plane, j)
            inv[plane, at, :] = value
            residual = r0[plane, at, :]
            precond = residual * value
            u0[plane, padded, :] = precond
            moment = moment + fold(residual * precond)
        return moment

    moment0 = lax.fori_loop(0, 32, first, none)
    send_plane(0, near_side)

    @pl.when(is_even)
    def _():
        def plain(t, carry):
            at = pl.ds(pl.multiple_of(t * TILE, TILE), TILE)
            shadow[at, :] = jnp.ones((TILE, cols), jnp.float32)
            return carry

        lax.fori_loop(0, steps, plain, 0)

    @pl.when(is_odd)
    def _():
        classify(depth + 2, depth, None)

        def beyond(j, carry):
            shadow[pl.ds(pl.multiple_of(j * words, words), words), :] = inverse(depth, j)
            return carry

        lax.fori_loop(0, 32, beyond, 0)
        if rounds:
            hear(0)

    def local_part(field, scaled, out, plane, start):
        at = pl.ds(start, TILE)
        _, total = inplane(field, plane, start)
        if plane > 0:
            total = total + centre_of(field, plane - 1, start)
        if plane < depth - 1:
            total = total + centre_of(field, plane + 1, start)
        image = jnp.where(inv[plane, at, :] > 0.0, scaled[plane, at, :] - total, 0.0)
        out[plane, at, :] = image
        return image

    def apply_once(plane, start, image, value, moments):
        precond = image * value
        put(u1, plane, start, precond)
        return (
            moments[0] + fold(image * centre_of(u0, plane, start)),
            moments[1] + fold(image * precond),
        )

    def second(t, moments):
        start = pl.multiple_of(t * TILE, TILE)
        for plane in range(depth):
            image = local_part(u0, r0, w0, plane, start)
            if 0 < plane < depth - 1:
                value = inv[plane, pl.ds(start, TILE), :]
                moments = apply_once(plane, start, image, value, moments)
        return moments

    moments = lax.fori_loop(0, steps, second, (none, none))

    def edge_one(side, moments):
        plane = side * (depth - 1)

        def step(k, moments):
            wait_halo(0, side, k)

            def tile(t, moments):
                start = row(k, t)
                at = pl.ds(start, TILE)
                value = inv[plane, at, :]
                beyond = halo_r[side, at, :]
                if side is far_side:
                    beyond = beyond * shadow[at, :]
                image = jnp.where(value > 0.0, w0[plane, at, :] - beyond, 0.0)
                w0[plane, at, :] = image
                return apply_once(plane, start, image, value, moments)

            moments = lax.fori_loop(0, tiles, tile, moments)
            if side is near_side:
                halo_copy(1, side, k).start()
            else:
                @pl.when(jnp.logical_and(is_odd, has_far))
                def _():
                    halo_copy(1, side, k).start()

            return moments

        return lax.fori_loop(0, chunks, step, moments)

    started = chunks - pieces(AFTER)
    passing = digit == near_size - 1

    @pl.when(is_even)
    def _():
        sent_plane(0, far_side, 0, started)

        @pl.when(passing)
        def _():
            sent_plane(0, far_side, started)

        pl.semaphore_signal(go, inc=1, device_id=(partner,), device_id_type=MESH)

    @pl.when(is_odd)
    def _():
        pl.semaphore_wait(go, 1)
        send_plane(0, far_side)

    moments = edge_one(near_side, moments)
    moment1, moment2 = edge_one(far_side, moments)

    def third(t, moment):
        start = pl.multiple_of(t * TILE, TILE)
        for plane in range(depth):
            image = local_part(u1, w0, w1, plane, start)
            moment = moment + fold(image * centre_of(u1, plane, start))
        return moment

    moment3 = lax.fori_loop(0, steps, third, none)

    def edge_two(side, moment, weight, after):
        plane = side * (depth - 1)

        def step(k, moment):
            wait_halo(1, side, k)
            after(k)

            def tile(t, moment):
                start = row(k, t)
                at = pl.ds(start, TILE)
                beyond = halo_u[side, at, :]
                image = jnp.where(inv[plane, at, :] > 0.0, w1[plane, at, :] - beyond, 0.0)
                w1[plane, at, :] = image
                return moment - weight * fold(beyond * centre_of(u1, plane, start))

            return lax.fori_loop(0, tiles, tile, moment)

        return lax.fori_loop(0, chunks, step, moment)

    def lanes(value):
        total = value[:, 0:128]
        for i in range(128, cols, 128):
            total = total + value[:, i:i + 128]
        return jnp.sum(total, axis=0, keepdims=True)

    def settle(moment):
        for i, value in enumerate((moment0, moment1, moment2, moment)):
            mine[0, i:i + 1, :] = lanes(value)
        mine[0, 4:8, :] = jnp.zeros((4, 128), jnp.float32)

    moment3 = edge_two(near_side, moment3, 1.0, lambda k: None)

    def pair_copy():
        return pltpu.make_async_remote_copy(
            src_ref=mine.at[0], dst_ref=pair, send_sem=pair_send, recv_sem=pair_recv,
            device_id=(partner,), device_id_type=MESH,
        )

    def sum_copy(stage, j, core, shift=0):
        slot, other = peer(stage, j)
        return pltpu.make_async_remote_copy(
            src_ref=mine.at[stage],
            dst_ref=got.at[stage, slot],
            send_sem=sum_send.at[core, stage + (shift > 0), j],
            recv_sem=sum_recv.at[stage, slot],
            device_id=(2 * (other - shift) + core,),
            device_id_type=MESH,
        )

    def across(act):
        act(sum_copy(1, 0, 0))

        def to_all(shift):
            for j in range(1, far_size):
                for core in (1, 0):
                    act(sum_copy(1, j, core, shift))

        if relief:
            pl.when(is_relief)(lambda: to_all(relief))
            pl.when(jnp.logical_not(is_first))(lambda: to_all(0))
        else:
            to_all(0)

    def sum_arrival(stage, slot):
        return pltpu.make_async_remote_copy(
            src_ref=got.at[stage, slot],
            dst_ref=got.at[stage, slot],
            send_sem=sum_send.at[0, stage, 0],
            recv_sem=sum_recv.at[stage, slot],
            device_id=(partner,),
            device_id_type=MESH,
        )

    def gathered(stage):
        total = got[stage, 0]
        for i in range(1, stages[stage][0]):
            total = total + got[stage, i]
        return total

    @pl.when(is_even)
    def _():
        def early(k):
            @pl.when(k == chunks - lag)
            def _():
                pl.semaphore_wait(go, 1)
                send_plane(1, far_side, 0, False, burst)

        settle(edge_two(far_side, moment3, 2.0, early))
        pair_copy().wait_recv()
        mine[0] = mine[0] + pair[...]
        for j in range(near_size):
            sum_copy(0, j, 1).start()

        @pl.when(has_far)
        def _():
            def pace(k, carry):
                halo_copy(1, 0, k - deep).wait_send()
                halo_copy(1, 0, k).start()
                return carry

            send_plane(1, far_side, burst, False, deep)
            lax.fori_loop(deep, chunks, pace, 0)

    @pl.when(is_odd)
    def _():
        settle(moment3)
        pair_copy().start()
        sent_plane(1, far_side, 0, chunks - hold)
        pl.semaphore_signal(go, inc=1, device_id=(partner,), device_id_type=MESH)
        for which in range(1, len(rounds)):
            hear(which)
        for i in range(near_size):
            sum_arrival(0, i).wait_recv()
        total = gathered(0)
        mine[1] = total
        across(lambda copy: copy.start())
        got[1, peer(1, 0)[0]] = total

    bit_copy(near_side, 1).wait_send()
    for phase in range(2):
        sent_plane(phase, near_side)

    @pl.when(is_even)
    def _():
        on(far_side, lambda: bit_copy(0, 2).wait_send())
        @pl.when(jnp.logical_not(passing))
        def _():
            sent_plane(0, far_side, started)

        for j in range(near_size):
            sum_copy(0, j, 1).wait_send()

    @pl.when(is_odd)
    def _():
        on(far_side, lambda: bit_copy(1, 1).wait_send())
        sent_plane(0, far_side)
        sent_plane(1, far_side, chunks - hold)
        pair_copy().wait_send()
        across(lambda copy: copy.wait_send())

    for j in range(1, far_size):
        sum_arrival(1, lax.rem(peer(1, 0)[0] + j, far_size)).wait_recv()
    @pl.when(is_even)
    def _():
        sum_arrival(1, peer(1, 0)[0]).wait_recv()

    everyone = gathered(1)
    s0, s1, s2, s3 = (everyone[i:i + 1] for i in range(4))

    def whole(value):
        return jnp.sum(value, axis=1, keepdims=True)

    rz_old = whole(s0)
    step_old = rz_old / whole(s1)
    rz_now = whole(s0 - 2.0 * step_old * s1 + step_old * step_old * s2)
    grown = 1.0 + rz_now / rz_old
    product = whole(grown * grown * s1 - 2.0 * step_old * grown * s2 + step_old * step_old * s3)
    step_size = rz_now / product
    lead = step_old + step_size * grown
    trail = step_size * step_old

    for plane in range(depth):
        def last(t, carry, plane=plane):
            at = pl.ds(pl.multiple_of(t * final, final), final)
            base = r0[plane, at, :]
            along = w0[plane, at, :]
            sol_ref[plane, at, :] = inv[plane, at, :] * (lead * base - trail * along)
            res_ref[plane, at, :] = base - lead * along + trail * w1[plane, at, :]
            return carry

        lax.fori_loop(0, rows // final, last, 0)

    @pl.when(jnp.logical_and(is_odd, has_far))
    def _():
        plane = depth - 1

        def late(k, carry):
            halo_arrival(1, 1, k).wait_recv()

            def tile(t, carry):
                at = pl.ds(row(k, t), TILE)
                beyond = jnp.where(inv[plane, at, :] > 0.0, halo_u[1, at, :], 0.0)
                res_ref[plane, at, :] = res_ref[plane, at, :] - trail * beyond
                return carry

            return lax.fori_loop(0, tiles, tile, carry)

        lax.fori_loop(0, chunks, late, 0)

    @pl.when(is_even)
    def _():
        sent_plane(1, far_side, chunks - deep)


def store(sol_ref, res_ref, sol_out, res_out, sem):
    copies = []
    for which, (source, target) in enumerate(((sol_ref, sol_out), (res_ref, res_out))):
        for plane in range(sol_ref.shape[0]):
            copies.append(
                pltpu.make_async_copy(source.at[plane], target.at[plane], sem.at[which, plane])
            )
    for copy in copies:
        copy.start()
    for copy in copies:
        copy.wait()


def groups(chips):
    near = math.gcd(chips, 4)
    return (near, 1), (chips // near, near)


def body(count, right_side, cell_flags):
    depth, rows, cols = right_side.shape
    assert count % 2 == 0 and depth > 1
    stages = groups(count // 2)
    widest = max(size for size, _ in stages)
    chunk = math.gcd(rows, CHUNK)
    chunks = rows // chunk
    f32 = jnp.float32
    field = pltpu.VMEM((depth, rows, cols), f32)
    padded = pltpu.VMEM((depth, rows + 2 * PAD, cols), f32)
    dma = pltpu.SemaphoreType.DMA
    grant = VMEM_BYTES - 8 * right_side.size - 2**19
    fields = pl.pallas_call(
        functools.partial(kernel, count, chunk, stages),
        out_shape=(field, field),
        in_specs=[pl.BlockSpec(memory_space=pltpu.HBM)] * 2,
        out_specs=(pl.BlockSpec(memory_space=pltpu.VMEM),) * 2,
        scratch_shapes=[
            field,
            pltpu.VMEM((depth, rows, cols), jnp.int32),
            field, field,
            pltpu.VMEM((rows, cols), f32),
            padded, padded, field, field,
            pltpu.VMEM((2, rows, cols), f32),
            pltpu.VMEM((2, rows, cols), f32),
            pltpu.VMEM((depth + 4, rows // 32, cols), jnp.int32),
            pltpu.VMEM((depth, rows // 32, cols), jnp.int32),
            pltpu.VMEM((depth + 1, 3, rows // 32, cols), jnp.int32),
            pltpu.VMEM((8, 128), f32),
            pltpu.VMEM((2, 8, 128), f32),
            pltpu.VMEM((2, widest, 8, 128), f32),
            dma((2, depth)),
            pltpu.SemaphoreType.REGULAR,
            pltpu.SemaphoreType.REGULAR((max(stages[1][0] - 1, 1),)),
            dma((2,)), dma((2,)),
            dma((2, 2, chunks)), dma((2, 2, chunks)),
            dma, dma,
            dma((2, 3, widest)), dma((2, widest)),
        ],
        compiler_params=pltpu.CompilerParams(
            collective_id=0, has_side_effects=True, vmem_limit_bytes=grant
        ),
    )(right_side, cell_flags)
    result = jax.ShapeDtypeStruct((depth, rows, cols), f32)
    return pl.pallas_call(
        store,
        out_shape=(result, result),
        in_specs=[pl.BlockSpec(memory_space=pltpu.VMEM)] * 2,
        out_specs=(pl.BlockSpec(memory_space=pltpu.HBM),) * 2,
        scratch_shapes=[dma((2, depth))],
        compiler_params=pltpu.CompilerParams(vmem_limit_bytes=2**19),
    )(*fields)


def solution(mesh):
    placed = (P("gz", None, None), P("gz", None, None))
    return jax.shard_map(
        functools.partial(body, mesh.shape["gz"]),
        mesh=mesh,
        in_specs=placed,
        out_specs=placed,
        check_vma=False,
    )
```

time: 59.1 us -> 56.1 us (0.949); the launches traced: 58.2 us -> 56 us
  local copies, waits for them, and re-layouts: 2.64 us -> 0 us
    unnamed x2 -> x0, local copies, waits for them, and re-layouts: 2.64 us -> none
    pallas_call x0 -> x1, Pallas kernels: none -> 2.04 us  [body(): pl.pallas_call(store, out_shape=(result, result), in_specs=[pl.BlockSpec(...]
    pallas_call x1, Pallas kernels: 54.9 us -> 53.3 us  [body(): pl.pallas_call(functools.partial(kernel, count, chunk, stages), out_shape...]
where the time goes in v3:
time: 56.1 us; the launch traced here: 56 us
  Pallas kernels  55.4 us (99%)
  between operations  0.64 us (1%)
    pallas_call x1, Pallas kernels, body(): pl.pallas_call(functools.partial(kernel, count, chunk, stages), out_shape...  53.3 us
    pallas_call x1, Pallas kernels, body(): pl.pallas_call(store, out_shape=(result, result), in_specs=[pl.BlockSpec(...  2.04 us

profile of v3, /device:TPU:1, one launch (start us, length us, event | category | flops | bytes accessed | tf_op | source)
XLA Modules:
  0.0 56.0 jit_solution(16356250394247534174)
XLA Ops:
  0.6 53.3 %shard_map.41 = (f32[2,512,512]{2,1,0:T(8,128)S(1)}, f32[2,512,512]{2,1,0:T(8,128)S(1)}) custom-call(f32[2,512,512]{2,1,0:T(8,128)} %side_hbm.1, s32[2,512,512]{2,1,0:T(8,128)} %flag_hbm.1), custom_call_target="tpu_custom_call" | custom-call | tf_op jit(solution)/shard_map/pallas_call | solution.py:683
  53.9 2.0 %shard_map.42 = (f32[2,512,512]{2,1,0:T(8,128)}, f32[2,512,512]{2,1,0:T(8,128)}) custom-call(f32[2,512,512]{2,1,0:T(8,128)S(1)} %get-tuple-element.4.sol_ref, f32[2,512,512]{2,1,0:T(8,128)S(1)} %get-tuple-element.5.res_ref), custom_call_target="tpu_custom_call" | custom-call | tf_op jit(solution)/shard_map/pallas_call | solution.py:715

commit v4 on v3

--- a/solution.py
+++ b/solution.py
@@ -15,7 +15,7 @@
 AFTER = 128
 LAGS = (192, 256)
 BURSTS = (128, 192)
-HOLDS = (64, 192)
+HOLDS = (64, 64)
 WINDOW = 256
 PAD = 8
 VMEM_BYTES = 67_043_328
@@ -26,7 +26,7 @@
     side_hbm, flag_hbm, sol_ref, res_ref,
     rhs, flags, r0, inv, shadow, u0, u1, w0, w1, halo_r, halo_u, solid, fluid, code,
     pair, mine, got,
-    in_sem, go, known, bit_send, bit_recv, halo_send, halo_recv,
+    in_sem, go, clear, known, bit_send, bit_recv, halo_send, halo_recv,
     pair_send, pair_recv, sum_send, sum_recv,
 ):
     depth, rows, cols = rhs.shape
@@ -79,9 +79,9 @@
     greet(partner)
     inner_planes = list(range(1, depth - 1))
     load(far_plane, 0).start()
+    load(far_plane, 1).start()
     for plane in [near_plane] + inner_planes:
         load(plane, 0).start()
-    load(far_plane, 1).start()
     for plane in [near_plane] + inner_planes:
         load(plane, 1).start()
     pairs = far_size & (far_size - 1) == 0
@@ -199,14 +199,15 @@
 
         on(side, all_chunks)
 
-    def bit_copy(side, planes, arrival=False):
-        mine_at, theirs_at = 2 + side * (depth - 1), 1 + (1 - side) * (depth + 1)
-        halo_at = 1 + side * (depth + 1)
+    def bit_copy(side, depth_in=0, arrival=False):
+        mine_at = 2 + side * (depth - 1) + depth_in * (1 - 2 * side)
+        theirs_at = 1 + (1 - side) * (depth + 1) + depth_in * (1 - 2 * side)
+        halo_at = 1 + side * (depth + 1) - depth_in * (1 - 2 * side)
         return pltpu.make_async_remote_copy(
-            src_ref=solid.at[pl.ds(halo_at if arrival else mine_at, planes)],
-            dst_ref=solid.at[pl.ds(halo_at if arrival else theirs_at, planes)],
-            send_sem=bit_send.at[side],
-            recv_sem=bit_recv.at[side if arrival else 1 - side],
+            src_ref=solid.at[halo_at if arrival else mine_at],
+            dst_ref=solid.at[halo_at if arrival else theirs_at],
+            send_sem=bit_send.at[side, depth_in],
+            recv_sem=bit_recv.at[side if arrival else 1 - side, depth_in],
             device_id=(me - 1 + 2 * side,),
             device_id_type=MESH,
         )
@@ -234,43 +235,52 @@
         empty = jnp.zeros((words, cols), jnp.int32)
         solid[plane + 2], fluid[plane] = lax.fori_loop(0, 32, one, (empty, empty))
 
-    for plane in [far_plane, near_plane] + inner_planes:
+    greeted = sum(len(group) for group in rounds) + near_size - 1 + (relief > 0)
+    callers = 1 + has_far.astype(jnp.int32)
+    reserve = jnp.where(is_first, pieces(AFTER), 0)
+    load(far_plane, 0).wait()
+    pack(far_plane)
+
+    @pl.when(is_even)
+    def _():
+        pl.semaphore_wait(barrier, callers)
+        on(far_side, lambda: bit_copy(0).start())
+
+    load(far_plane, 1).wait()
+    mask(far_plane, 0, tiles)
+
+    @pl.when(is_even)
+    def _():
+        on(far_side, lambda: halo_copy(0, 0, 0, True).start())
+
+    for plane in [near_plane] + inner_planes:
         load(plane, 0).wait()
         pack(plane)
-    greeted = sum(len(group) for group in rounds) + near_size - 1 + (relief > 0)
-    pl.semaphore_wait(barrier, 1 + has_far.astype(jnp.int32) + odd * greeted)
-
-    @pl.when(is_even)
-    def _():
-        on(far_side, lambda: bit_copy(0, 2).start())
+
+    @pl.when(is_even)
+    def _():
+        on(far_side, lambda: bit_copy(0, 1).start())
 
     @pl.when(is_odd)
     def _():
-        on(far_side, lambda: bit_copy(1, 1).start())
+        pl.semaphore_wait(barrier, callers + greeted)
+        on(far_side, lambda: bit_copy(1).start())
         if rounds:
             tell(0)
 
-    bit_copy(near_side, 1).start()
-    load(far_plane, 1).wait()
-    mask(far_plane, 0, steps)
-
-    @pl.when(is_even)
-    def _():
-        send_plane(0, far_side, 0, True)
+    bit_copy(near_side).start()
+    mask(far_plane, tiles, steps)
+
+    @pl.when(is_even)
+    def _():
+        send_plane(0, far_side, 1, True, chunks - reserve)
 
     for plane in [near_plane] + inner_planes:
         load(plane, 1).wait()
         mask(plane, 0, steps)
 
-    bit_copy(near_side, 1, True).wait_recv()
-
-    @pl.when(is_even)
-    def _():
-        on(far_side, lambda: bit_copy(0, 1, True).wait_recv())
-
-    @pl.when(is_odd)
-    def _():
-        on(far_side, lambda: bit_copy(1, 2, True).wait_recv())
+    bit_copy(near_side, 0, True).wait_recv()
+    on(far_side, lambda: bit_copy(far_side, 0, True).wait_recv())
 
     def classify(at, slot, known_fluid):
         word = solid[at]
@@ -346,6 +356,10 @@
     moment0 = lax.fori_loop(0, 32, first, none)
     send_plane(0, near_side)
 
+    @pl.when(jnp.logical_and(is_odd, is_first))
+    def _():
+        send_plane(0, far_side)
+
     @pl.when(is_even)
     def _():
         def plain(t, carry):
@@ -357,6 +371,7 @@
 
     @pl.when(is_odd)
     def _():
+        on(far_side, lambda: bit_copy(1, 1, True).wait_recv())
         classify(depth + 2, depth, None)
 
         def beyond(j, carry):
@@ -426,23 +441,42 @@
 
         return lax.fori_loop(0, chunks, step, moments)
 
-    started = chunks - pieces(AFTER)
     passing = digit == near_size - 1
-
-    @pl.when(is_even)
-    def _():
-        sent_plane(0, far_side, 0, started)
-
-        @pl.when(passing)
+    started = jnp.where(
+        is_first, 0, chunks - jnp.where(passing, pieces(CHUNK), pieces(AFTER))
+    )
+
+    @pl.when(is_odd)
+    def _():
+        for which in range(1, len(rounds)):
+            hear(which)
+
+    @pl.when(jnp.logical_and(is_even, is_first))
+    def _():
+        send_plane(0, far_side, chunks - reserve, True)
+
+    @pl.when(jnp.logical_not(is_first))
+    def _():
+        @pl.when(is_even)
         def _():
-            sent_plane(0, far_side, started)
-
-        pl.semaphore_signal(go, inc=1, device_id=(partner,), device_id_type=MESH)
-
-    @pl.when(is_odd)
-    def _():
-        pl.semaphore_wait(go, 1)
-        send_plane(0, far_side)
+            sent_plane(0, far_side, 0, started)
+            pl.semaphore_signal(go, inc=1, device_id=(partner,), device_id_type=MESH)
+
+        @pl.when(is_odd)
+        def _():
+            pl.semaphore_wait(go, 1)
+
+            @pl.when(jnp.logical_and(passing, chip >= near_size))
+            def _():
+                pl.semaphore_signal(
+                    clear, inc=1, device_id=(me - 2 * near_size,), device_id_type=MESH
+                )
+
+            @pl.when(jnp.logical_and(passing, chip + near_size < count // 2))
+            def _():
+                pl.semaphore_wait(clear, 1)
+
+            send_plane(0, far_side)
 
     moments = edge_one(near_side, moments)
     moment1, moment2 = edge_one(far_side, moments)
@@ -481,11 +515,9 @@
             total = total + value[:, i:i + 128]
         return jnp.sum(total, axis=0, keepdims=True)
 
-    def settle(moment):
-        for i, value in enumerate((moment0, moment1, moment2, moment)):
-            mine[0, i:i + 1, :] = lanes(value)
-        mine[0, 4:8, :] = jnp.zeros((4, 128), jnp.float32)
-
+    for i, value in enumerate((moment0, moment1, moment2)):
+        mine[0, i:i + 1, :] = lanes(value)
+    mine[0, 3:8, :] = jnp.zeros((5, 128), jnp.float32)
     moment3 = edge_two(near_side, moment3, 1.0, lambda k: None)
 
     def pair_copy():
@@ -540,12 +572,16 @@
         def early(k):
             @pl.when(k == chunks - lag)
             def _():
-                pl.semaphore_wait(go, 1)
+                @pl.when(jnp.logical_or(jnp.logical_not(is_first), chip >= near_size))
+                def _():
+                    pl.semaphore_wait(go, 1)
+
                 send_plane(1, far_side, 0, False, burst)
 
-        settle(edge_two(far_side, moment3, 2.0, early))
         pair_copy().wait_recv()
         mine[0] = mine[0] + pair[...]
+        moment = edge_two(far_side, moment3, 2.0, early)
+        mine[0, 3:4, :] = mine[0, 3:4, :] + lanes(moment)
         for j in range(near_size):
             sum_copy(0, j, 1).start()
 
@@ -561,12 +597,15 @@
 
     @pl.when(is_odd)
     def _():
-        settle(moment3)
+        mine[0, 3:4, :] = lanes(moment3)
         pair_copy().start()
         sent_plane(1, far_side, 0, chunks - hold)
-        pl.semaphore_signal(go, inc=1, device_id=(partner,), device_id_type=MESH)
-        for which in range(1, len(rounds)):
-            hear(which)
+
+        @pl.when(jnp.logical_or(jnp.logical_not(is_first), chip + near_size < count // 2))
+        def _():
+            waiting = jnp.where(is_first, me - 1 + 2 * near_size, partner)
+            pl.semaphore_signal(go, inc=1, device_id=(waiting,), device_id_type=MESH)
+
         for i in range(near_size):
             sum_arrival(0, i).wait_recv()
         total = gathered(0)
@@ -574,23 +613,20 @@
         across(lambda copy: copy.start())
         got[1, peer(1, 0)[0]] = total
 
-    bit_copy(near_side, 1).wait_send()
+    bit_copy(near_side).wait_send()
+    on(far_side, lambda: bit_copy(far_side).wait_send())
     for phase in range(2):
         sent_plane(phase, near_side)
 
     @pl.when(is_even)
     def _():
-        on(far_side, lambda: bit_copy(0, 2).wait_send())
-        @pl.when(jnp.logical_not(passing))
-        def _():
-            sent_plane(0, far_side, started)
-
+        on(far_side, lambda: bit_copy(0, 1).wait_send())
+        sent_plane(0, far_side, started)
         for j in range(near_size):
             sum_copy(0, j, 1).wait_send()
 
     @pl.when(is_odd)
     def _():
-        on(far_side, lambda: bit_copy(1, 1).wait_send())
         sent_plane(0, far_side)
         sent_plane(1, far_side, chunks - hold)
         pair_copy().wait_send()
@@ -701,8 +737,9 @@
             pltpu.VMEM((2, widest, 8, 128), f32),
             dma((2, depth)),
             pltpu.SemaphoreType.REGULAR,
+            pltpu.SemaphoreType.REGULAR,
             pltpu.SemaphoreType.REGULAR((max(stages[1][0] - 1, 1),)),
-            dma((2,)), dma((2,)),
+            dma((2, 2)), dma((2, 2)),
             dma((2, 2, chunks)), dma((2, 2, chunks)),
             dma, dma,
             dma((2, 3, widest)), dma((2, widest)),

time: 56.1 us -> 55.7 us (level)
  no operation moved by 1% of the time
where the time goes in v4:
time: 55.7 us; the launch traced here: 55.5 us
  Pallas kernels  54.9 us (99%)
  between operations  0.64 us (1%)
    pallas_call x1, Pallas kernels, body(): pl.pallas_call(functools.partial(kernel, count, chunk, stages), out_shape...  52.9 us
    pallas_call x1, Pallas kernels, body(): pl.pallas_call(store, out_shape=(result, result), in_specs=[pl.BlockSpec(...  2.04 us

profile of v4, /device:TPU:1, one launch (start us, length us, event | category | flops | bytes accessed | tf_op | source)
XLA Modules:
  0.0 55.5 jit_solution(14883962362503133922)
XLA Ops:
  0.6 52.9 %shard_map.41 = (f32[2,512,512]{2,1,0:T(8,128)S(1)}, f32[2,512,512]{2,1,0:T(8,128)S(1)}) custom-call(f32[2,512,512]{2,1,0:T(8,128)} %side_hbm.1, s32[2,512,512]{2,1,0:T(8,128)} %flag_hbm.1), custom_call_target="tpu_custom_call" | custom-call | tf_op jit(solution)/shard_map/pallas_call | solution.py:719
  53.5 2.0 %shard_map.42 = (f32[2,512,512]{2,1,0:T(8,128)}, f32[2,512,512]{2,1,0:T(8,128)}) custom-call(f32[2,512,512]{2,1,0:T(8,128)S(1)} %get-tuple-element.4.sol_ref, f32[2,512,512]{2,1,0:T(8,128)S(1)} %get-tuple-element.5.res_ref), custom_call_target="tpu_custom_call" | custom-call | tf_op jit(solution)/shard_map/pallas_call | solution.py:752

commit v5 on v4

--- a/solution.py
+++ b/solution.py
@@ -11,12 +11,8 @@
 MESH = pl.DeviceIdType.MESH
 TILE = 16
 LAST = 64
+LATE = (0, 2, 3, 5, 7, 8)
 CHUNK = 64
-AFTER = 128
-LAGS = (192, 256)
-BURSTS = (128, 192)
-HOLDS = (64, 64)
-WINDOW = 256
 PAD = 8
 VMEM_BYTES = 67_043_328
 
@@ -26,19 +22,18 @@
     side_hbm, flag_hbm, sol_ref, res_ref,
     rhs, flags, r0, inv, shadow, u0, u1, w0, w1, halo_r, halo_u, solid, fluid, code,
     pair, mine, got,
-    in_sem, go, clear, known, bit_send, bit_recv, halo_send, halo_recv,
+    in_sem, go, clear, known, bit_send, bit_recv, far_send, far_recv, near_send, near_recv,
     pair_send, pair_recv, sum_send, sum_recv,
 ):
     depth, rows, cols = rhs.shape
     words = rows // 32
-    chunks = rows // chunk
-    tiles = chunk // TILE
     steps = rows // TILE
-
-    def pieces(length):
-        return min(max(length // chunk, 1), chunks)
-
-    deep = pieces(WINDOW)
+    parts = rows // chunk
+    marks = sorted({0, 1, max(parts - 3, 0), max(parts - 2, 0), max(parts - 1, 0), parts})
+    spans = [(a * chunk, (b - a) * chunk) for a, b in zip(marks, marks[1:])]
+    most = (0, rows - spans[-1][1])
+    late_marks = [rows * eighth // 8 for eighth in LATE]
+    lates = [(a, b - a) for a, b in zip(late_marks, late_marks[1:])]
     final = math.gcd(rows, LAST)
     near_size, far_size = stages[0][0], stages[1][0]
     me = lax.axis_index("gz")
@@ -52,11 +47,6 @@
     digit = lax.rem(chip, near_size)
     relief = near_size // 2 if near_size > 2 else 0
     is_first, is_relief = digit == 0, digit == relief
-
-    def by_place(lengths):
-        return jnp.where(is_first, pieces(lengths[1]), pieces(lengths[0]))
-
-    lag, burst, hold = by_place(LAGS), by_place(BURSTS), by_place(HOLDS)
 
     def load(plane, which):
         source, target = ((flag_hbm, flags), (side_hbm, rhs))[which]
@@ -147,57 +137,64 @@
         else:
             there()
 
-    def halo_copy(phase, side, k, raw=False):
-        at = pl.multiple_of(k * chunk, chunk)
+    def halo_copy(phase, side, span, send, recv, raw=False):
+        start, size = span
         plane = side * (depth - 1)
         if raw:
-            source = r0.at[plane, pl.ds(at, chunk)]
+            source = r0.at[plane, pl.ds(start, size)]
         else:
-            field = (u0, u1)[phase]
-            source = field.at[plane, pl.ds(pl.multiple_of(at + PAD, PAD), chunk)]
+            source = (u0, u1)[phase].at[plane, pl.ds(start + PAD, size)]
         return pltpu.make_async_remote_copy(
             src_ref=source,
-            dst_ref=(halo_r, halo_u)[phase].at[1 - side, pl.ds(at, chunk)],
-            send_sem=halo_send.at[phase, side, k],
-            recv_sem=halo_recv.at[phase, 1 - side, k],
+            dst_ref=(halo_r, halo_u)[phase].at[1 - side, pl.ds(start, size)],
+            send_sem=send,
+            recv_sem=recv,
             device_id=(me - 1 + 2 * side,),
             device_id_type=MESH,
         )
 
-    def halo_arrival(phase, side, k):
-        at = pl.multiple_of(k * chunk, chunk)
-        target = (halo_r, halo_u)[phase].at[side, pl.ds(at, chunk)]
+    def halo_arrival(phase, side, span, recv):
+        start, size = span
+        target = (halo_r, halo_u)[phase].at[side, pl.ds(start, size)]
         return pltpu.make_async_remote_copy(
             src_ref=target,
             dst_ref=target,
-            send_sem=halo_send.at[phase, side, k],
-            recv_sem=halo_recv.at[phase, side, k],
+            send_sem=near_send.at[phase],
+            recv_sem=recv,
             device_id=(me - 1 + 2 * side,),
             device_id_type=MESH,
         )
 
-    def wait_halo(phase, side, k):
-        on(side, lambda: halo_arrival(phase, side, k).wait_recv())
-
-    def send_plane(phase, side, first=0, raw=False, last=chunks):
-        def all_chunks():
-            def one(k, carry):
-                halo_copy(phase, side, k, raw).start()
-                return carry
-
-            lax.fori_loop(first, last, one, 0)
-
-        on(side, all_chunks)
-
-    def sent_plane(phase, side, first=0, last=chunks):
-        def all_chunks():
-            def one(k, carry):
-                halo_copy(phase, side, k).wait_send()
-                return carry
-
-            lax.fori_loop(first, last, one, 0)
-
-        on(side, all_chunks)
+    def far_copy(phase, i, raw=False):
+        send = far_send.at[2 * phase + (i == len(spans) - 1)]
+        return halo_copy(phase, far_side, spans[i], send, far_recv.at[phase, i], raw)
+
+    def far_sent(phase):
+        sender = far_send.at[2 * phase]
+        on(far_side, lambda: halo_copy(
+            phase, far_side, most, sender, far_recv.at[phase, 0]
+        ).wait_send())
+
+    def far_ended(phase):
+        on(far_side, lambda: far_copy(phase, len(spans) - 1).wait_send())
+
+    def late_copy(i):
+        return halo_copy(1, far_side, lates[i], far_send.at[2 + i], far_recv.at[1, i])
+
+    def near_copy(phase):
+        return halo_copy(
+            phase, near_side, (0, rows), near_send.at[phase], near_recv.at[phase]
+        )
+
+    def near_arrival(phase):
+        return halo_arrival(phase, near_side, (0, rows), near_recv.at[phase])
+
+    def far_pieces(first, last, phase=0, raw=False):
+        def some():
+            for i in range(first, last):
+                far_copy(phase, i, raw).start()
+
+        on(far_side, some)
 
     def bit_copy(side, depth_in=0, arrival=False):
         mine_at = 2 + side * (depth - 1) + depth_in * (1 - 2 * side)
@@ -206,14 +203,22 @@
         return pltpu.make_async_remote_copy(
             src_ref=solid.at[halo_at if arrival else mine_at],
             dst_ref=solid.at[halo_at if arrival else theirs_at],
-            send_sem=bit_send.at[side, depth_in],
-            recv_sem=bit_recv.at[side if arrival else 1 - side, depth_in],
+            send_sem=bit_send,
+            recv_sem=bit_recv.at[2 if depth_in else side if arrival else 1 - side],
             device_id=(me - 1 + 2 * side,),
             device_id_type=MESH,
         )
 
-    def row(k, t):
-        return pl.multiple_of(k * chunk + t * TILE, TILE)
+    def bits_sent(planes):
+        several = solid.at[pl.ds(0, planes)]
+        pltpu.make_async_remote_copy(
+            src_ref=several,
+            dst_ref=several,
+            send_sem=bit_send,
+            recv_sem=bit_recv.at[0],
+            device_id=(partner,),
+            device_id_type=MESH,
+        ).wait_send()
 
     def mask(plane, first, last):
         def tile(t, carry):
@@ -237,7 +242,7 @@
 
     greeted = sum(len(group) for group in rounds) + near_size - 1 + (relief > 0)
     callers = 1 + has_far.astype(jnp.int32)
-    reserve = jnp.where(is_first, pieces(AFTER), 0)
+    kept = max(len(spans) - 2, 1)
     load(far_plane, 0).wait()
     pack(far_plane)
 
@@ -247,11 +252,11 @@
         on(far_side, lambda: bit_copy(0).start())
 
     load(far_plane, 1).wait()
-    mask(far_plane, 0, tiles)
+    mask(far_plane, 0, chunk // TILE)
 
     @pl.when(is_even)
     def _():
-        on(far_side, lambda: halo_copy(0, 0, 0, True).start())
+        far_pieces(0, 1, raw=True)
 
     for plane in [near_plane] + inner_planes:
         load(plane, 0).wait()
@@ -269,11 +274,15 @@
             tell(0)
 
     bit_copy(near_side).start()
-    mask(far_plane, tiles, steps)
+    mask(far_plane, chunk // TILE, steps)
 
     @pl.when(is_even)
     def _():
-        send_plane(0, far_side, 1, True, chunks - reserve)
+        far_pieces(1, kept, raw=True)
+
+        @pl.when(jnp.logical_not(is_first))
+        def _():
+            far_pieces(kept, len(spans), raw=True)
 
     for plane in [near_plane] + inner_planes:
         load(plane, 1).wait()
@@ -354,11 +363,11 @@
         return moment
 
     moment0 = lax.fori_loop(0, 32, first, none)
-    send_plane(0, near_side)
+    near_copy(0).start()
 
     @pl.when(jnp.logical_and(is_odd, is_first))
     def _():
-        send_plane(0, far_side)
+        far_pieces(0, len(spans))
 
     @pl.when(is_even)
     def _():
@@ -412,40 +421,23 @@
 
     moments = lax.fori_loop(0, steps, second, (none, none))
 
-    def edge_one(side, moments):
+    def edge_one(side, span, moments):
         plane = side * (depth - 1)
 
-        def step(k, moments):
-            wait_halo(0, side, k)
-
-            def tile(t, moments):
-                start = row(k, t)
-                at = pl.ds(start, TILE)
-                value = inv[plane, at, :]
-                beyond = halo_r[side, at, :]
-                if side is far_side:
-                    beyond = beyond * shadow[at, :]
-                image = jnp.where(value > 0.0, w0[plane, at, :] - beyond, 0.0)
-                w0[plane, at, :] = image
-                return apply_once(plane, start, image, value, moments)
-
-            moments = lax.fori_loop(0, tiles, tile, moments)
-            if side is near_side:
-                halo_copy(1, side, k).start()
-            else:
-                @pl.when(jnp.logical_and(is_odd, has_far))
-                def _():
-                    halo_copy(1, side, k).start()
-
-            return moments
-
-        return lax.fori_loop(0, chunks, step, moments)
+        def tile(t, moments):
+            start = pl.multiple_of(span[0] + t * TILE, TILE)
+            at = pl.ds(start, TILE)
+            value = inv[plane, at, :]
+            beyond = halo_r[side, at, :]
+            if side is far_side:
+                beyond = beyond * shadow[at, :]
+            image = jnp.where(value > 0.0, w0[plane, at, :] - beyond, 0.0)
+            w0[plane, at, :] = image
+            return apply_once(plane, start, image, value, moments)
+
+        return lax.fori_loop(0, span[1] // TILE, tile, moments)
 
     passing = digit == near_size - 1
-    started = jnp.where(
-        is_first, 0, chunks - jnp.where(passing, pieces(CHUNK), pieces(AFTER))
-    )
-
     @pl.when(is_odd)
     def _():
         for which in range(1, len(rounds)):
@@ -453,13 +445,13 @@
 
     @pl.when(jnp.logical_and(is_even, is_first))
     def _():
-        send_plane(0, far_side, chunks - reserve, True)
+        far_pieces(kept, len(spans), raw=True)
 
     @pl.when(jnp.logical_not(is_first))
     def _():
         @pl.when(is_even)
         def _():
-            sent_plane(0, far_side, 0, started)
+            far_sent(0)
             pl.semaphore_signal(go, inc=1, device_id=(partner,), device_id_type=MESH)
 
         @pl.when(is_odd)
@@ -476,10 +468,20 @@
             def _():
                 pl.semaphore_wait(clear, 1)
 
-            send_plane(0, far_side)
-
-    moments = edge_one(near_side, moments)
-    moment1, moment2 = edge_one(far_side, moments)
+            far_pieces(0, len(spans))
+
+    near_arrival(0).wait_recv()
+    moments = edge_one(near_side, (0, rows), moments)
+    near_copy(1).start()
+    for i, span in enumerate(spans):
+        on(far_side, lambda: halo_arrival(0, far_side, span, far_recv.at[0, i]).wait_recv())
+        moments = edge_one(far_side, span, moments)
+
+        @pl.when(is_odd)
+        def _():
+            far_pieces(i, i + 1, 1)
+
+    moment1, moment2 = moments
 
     def third(t, moment):
         start = pl.multiple_of(t * TILE, TILE)
@@ -490,24 +492,18 @@
 
     moment3 = lax.fori_loop(0, steps, third, none)
 
-    def edge_two(side, moment, weight, after):
+    def edge_two(side, span, moment, weight):
         plane = side * (depth - 1)
 
-        def step(k, moment):
-            wait_halo(1, side, k)
-            after(k)
-
-            def tile(t, moment):
-                start = row(k, t)
-                at = pl.ds(start, TILE)
-                beyond = halo_u[side, at, :]
-                image = jnp.where(inv[plane, at, :] > 0.0, w1[plane, at, :] - beyond, 0.0)
-                w1[plane, at, :] = image
-                return moment - weight * fold(beyond * centre_of(u1, plane, start))
-
-            return lax.fori_loop(0, tiles, tile, moment)
-
-        return lax.fori_loop(0, chunks, step, moment)
+        def tile(t, moment):
+            start = pl.multiple_of(span[0] + t * TILE, TILE)
+            at = pl.ds(start, TILE)
+            beyond = halo_u[side, at, :]
+            image = jnp.where(inv[plane, at, :] > 0.0, w1[plane, at, :] - beyond, 0.0)
+            w1[plane, at, :] = image
+            return moment - weight * fold(beyond * centre_of(u1, plane, start))
+
+        return lax.fori_loop(0, span[1] // TILE, tile, moment)
 
     def lanes(value):
         total = value[:, 0:128]
@@ -518,7 +514,8 @@
     for i, value in enumerate((moment0, moment1, moment2)):
         mine[0, i:i + 1, :] = lanes(value)
     mine[0, 3:8, :] = jnp.zeros((5, 128), jnp.float32)
-    moment3 = edge_two(near_side, moment3, 1.0, lambda k: None)
+    near_arrival(1).wait_recv()
+    moment3 = edge_two(near_side, (0, rows), moment3, 1.0)
 
     def pair_copy():
         return pltpu.make_async_remote_copy(
@@ -531,19 +528,30 @@
         return pltpu.make_async_remote_copy(
             src_ref=mine.at[stage],
             dst_ref=got.at[stage, slot],
-            send_sem=sum_send.at[core, stage + (shift > 0), j],
-            recv_sem=sum_recv.at[stage, slot],
+            send_sem=sum_send.at[0 if stage == 0 or j == 0 else 2 if shift else 1],
+            recv_sem=sum_recv.at[stage],
             device_id=(2 * (other - shift) + core,),
             device_id_type=MESH,
         )
 
-    def across(act):
-        act(sum_copy(1, 0, 0))
+    def sums(stage, copies, sender=0):
+        several = got.at[stage, pl.ds(0, copies)]
+        return pltpu.make_async_remote_copy(
+            src_ref=several,
+            dst_ref=several,
+            send_sem=sum_send.at[sender],
+            recv_sem=sum_recv.at[stage],
+            device_id=(partner,),
+            device_id_type=MESH,
+        )
+
+    def across():
+        sum_copy(1, 0, 0).start()
 
         def to_all(shift):
             for j in range(1, far_size):
                 for core in (1, 0):
-                    act(sum_copy(1, j, core, shift))
+                    sum_copy(1, j, core, shift).start()
 
         if relief:
             pl.when(is_relief)(lambda: to_all(relief))
@@ -551,15 +559,14 @@
         else:
             to_all(0)
 
-    def sum_arrival(stage, slot):
-        return pltpu.make_async_remote_copy(
-            src_ref=got.at[stage, slot],
-            dst_ref=got.at[stage, slot],
-            send_sem=sum_send.at[0, stage, 0],
-            recv_sem=sum_recv.at[stage, slot],
-            device_id=(partner,),
-            device_id_type=MESH,
-        )
+    def across_sent():
+        sums(0, 1).wait_send()
+        if far_size > 1:
+            pl.when(jnp.logical_not(is_first) if relief else True)(
+                lambda: sums(0, 2 * (far_size - 1), 1).wait_send()
+            )
+            if relief:
+                pl.when(is_relief)(lambda: sums(0, 2 * (far_size - 1), 2).wait_send())
 
     def gathered(stage):
         total = got[stage, 0]
@@ -569,74 +576,78 @@
 
     @pl.when(is_even)
     def _():
-        def early(k):
-            @pl.when(k == chunks - lag)
-            def _():
-                @pl.when(jnp.logical_or(jnp.logical_not(is_first), chip >= near_size))
-                def _():
-                    pl.semaphore_wait(go, 1)
-
-                send_plane(1, far_side, 0, False, burst)
-
         pair_copy().wait_recv()
         mine[0] = mine[0] + pair[...]
-        moment = edge_two(far_side, moment3, 2.0, early)
+        moment = moment3
+        for i, span in enumerate(spans):
+            on(far_side, lambda: halo_arrival(1, far_side, span, far_recv.at[1, i]).wait_recv())
+            for place, after in ((is_first, 4), (jnp.logical_not(is_first), 3)):
+                if i == max(len(spans) - after, 0):
+                    @pl.when(place)
+                    def _():
+                        @pl.when(jnp.logical_or(jnp.logical_not(is_first), chip >= near_size))
+                        def _():
+                            pl.semaphore_wait(go, 1)
+
+                        on(far_side, lambda: late_copy(0).start())
+
+                        @pl.when(jnp.logical_and(is_first, has_far))
+                        def _():
+                            late_copy(1).start()
+
+            moment = edge_two(far_side, span, moment, 2.0)
+
         mine[0, 3:4, :] = mine[0, 3:4, :] + lanes(moment)
         for j in range(near_size):
             sum_copy(0, j, 1).start()
 
         @pl.when(has_far)
         def _():
-            def pace(k, carry):
-                halo_copy(1, 0, k - deep).wait_send()
-                halo_copy(1, 0, k).start()
-                return carry
-
-            send_plane(1, far_side, burst, False, deep)
-            lax.fori_loop(deep, chunks, pace, 0)
+            pl.when(jnp.logical_not(is_first))(lambda: late_copy(1).start())
+            late_copy(2).start()
+            for i in range(3, len(lates)):
+                late_copy(i - 3).wait_send()
+                late_copy(i).start()
 
     @pl.when(is_odd)
     def _():
         mine[0, 3:4, :] = lanes(moment3)
         pair_copy().start()
-        sent_plane(1, far_side, 0, chunks - hold)
+        far_sent(1)
 
         @pl.when(jnp.logical_or(jnp.logical_not(is_first), chip + near_size < count // 2))
         def _():
             waiting = jnp.where(is_first, me - 1 + 2 * near_size, partner)
             pl.semaphore_signal(go, inc=1, device_id=(waiting,), device_id_type=MESH)
 
-        for i in range(near_size):
-            sum_arrival(0, i).wait_recv()
+        sums(0, near_size).wait_recv()
         total = gathered(0)
         mine[1] = total
-        across(lambda copy: copy.start())
+        across()
         got[1, peer(1, 0)[0]] = total
 
-    bit_copy(near_side).wait_send()
-    on(far_side, lambda: bit_copy(far_side).wait_send())
-    for phase in range(2):
-        sent_plane(phase, near_side)
+    near_copy(0).wait_send()
+    near_copy(1).wait_send()
+    far_ended(0)
 
     @pl.when(is_even)
     def _():
-        on(far_side, lambda: bit_copy(0, 1).wait_send())
-        sent_plane(0, far_side, started)
-        for j in range(near_size):
-            sum_copy(0, j, 1).wait_send()
+        pl.when(has_far)(lambda: bits_sent(3))
+        pl.when(jnp.logical_not(has_far))(lambda: bits_sent(1))
+        pl.when(is_first)(lambda: far_sent(0))
+        sums(0, near_size).wait_send()
+        sums(1, far_size).wait_recv()
 
     @pl.when(is_odd)
     def _():
-        sent_plane(0, far_side)
-        sent_plane(1, far_side, chunks - hold)
+        pl.when(has_far)(lambda: bits_sent(2))
+        pl.when(jnp.logical_not(has_far))(lambda: bits_sent(1))
+        far_sent(0)
+        far_ended(1)
         pair_copy().wait_send()
-        across(lambda copy: copy.wait_send())
-
-    for j in range(1, far_size):
-        sum_arrival(1, lax.rem(peer(1, 0)[0] + j, far_size)).wait_recv()
-    @pl.when(is_even)
-    def _():
-        sum_arrival(1, peer(1, 0)[0]).wait_recv()
+        across_sent()
+        if far_size > 1:
+            sums(1, far_size - 1).wait_recv()
 
     everyone = gathered(1)
     s0, s1, s2, s3 = (everyone[i:i + 1] for i in range(4))
@@ -668,22 +679,21 @@
     def _():
         plane = depth - 1
 
-        def late(k, carry):
-            halo_arrival(1, 1, k).wait_recv()
-
-            def tile(t, carry):
-                at = pl.ds(row(k, t), TILE)
+        for i, span in enumerate(lates):
+            halo_arrival(1, 1, span, far_recv.at[1, i]).wait_recv()
+
+            def tile(t, carry, span=span):
+                at = pl.ds(pl.multiple_of(span[0] + t * TILE, TILE), TILE)
                 beyond = jnp.where(inv[plane, at, :] > 0.0, halo_u[1, at, :], 0.0)
                 res_ref[plane, at, :] = res_ref[plane, at, :] - trail * beyond
                 return carry
 
-            return lax.fori_loop(0, tiles, tile, carry)
-
-        lax.fori_loop(0, chunks, late, 0)
-
-    @pl.when(is_even)
-    def _():
-        sent_plane(1, far_side, chunks - deep)
+            lax.fori_loop(0, span[1] // TILE, tile, 0)
+
+    @pl.when(jnp.logical_and(is_even, has_far))
+    def _():
+        for i in range(len(lates) - 3, len(lates)):
+            late_copy(i).wait_send()
 
 
 def store(sol_ref, res_ref, sol_out, res_out, sem):
@@ -708,9 +718,10 @@
     depth, rows, cols = right_side.shape
     assert count % 2 == 0 and depth > 1
     stages = groups(count // 2)
-    widest = max(size for size, _ in stages)
+    widest = max(stages[0][0], stages[1][0], 2 * (stages[1][0] - 1))
     chunk = math.gcd(rows, CHUNK)
-    chunks = rows // chunk
+    assert rows % (8 * TILE) == 0
+    pieces = max(len({0, 1, *(max(rows // chunk - i, 0) for i in range(4))}), len(LATE)) - 1
     f32 = jnp.float32
     field = pltpu.VMEM((depth, rows, cols), f32)
     padded = pltpu.VMEM((depth, rows + 2 * PAD, cols), f32)
@@ -738,11 +749,11 @@
             dma((2, depth)),
             pltpu.SemaphoreType.REGULAR,
             pltpu.SemaphoreType.REGULAR,
-            pltpu.SemaphoreType.REGULAR((max(stages[1][0] - 1, 1),)),
-            dma((2, 2)), dma((2, 2)),
-            dma((2, 2, chunks)), dma((2, 2, chunks)),
+            pltpu.SemaphoreType.REGULAR((max((stages[1][0] - 1).bit_length(), 1),)),
+            dma, dma((3,)),
+            dma((1 + len(LATE),)), dma((2, pieces)), dma((2,)), dma((2,)),
             dma, dma,
-            dma((2, 3, widest)), dma((2, widest)),
+            dma((3,)), dma((2,)),
         ],
         compiler_params=pltpu.CompilerParams(
             collective_id=0, has_side_effects=True, vmem_limit_bytes=grant

time: 55.7 us -> 55 us (0.987)
  Pallas kernels: 54.9 us -> 54.2 us
    pallas_call x1, Pallas kernels: 52.9 us -> 52.2 us  [body(): pl.pallas_call(functools.partial(kernel, count, chunk, stages), out_shape...]
where the time goes in v5:
time: 55 us; the launch traced here: 54.9 us
  Pallas kernels  54.2 us (99%)
  between operations  0.64 us (1%)
    pallas_call x1, Pallas kernels, body(): pl.pallas_call(functools.partial(kernel, count, chunk, stages), out_shape...  52.2 us
    pallas_call x1, Pallas kernels, body(): pl.pallas_call(store, out_shape=(result, result), in_specs=[pl.BlockSpec(...  2.04 us

profile of v5, /device:TPU:1, one launch (start us, length us, event | category | flops | bytes accessed | tf_op | source)
XLA Modules:
  0.0 54.9 jit_solution(10685299116655812506)
XLA Ops:
  0.6 52.2 %shard_map.41 = (f32[2,512,512]{2,1,0:T(8,128)S(1)}, f32[2,512,512]{2,1,0:T(8,128)S(1)}) custom-call(f32[2,512,512]{2,1,0:T(8,128)} %side_hbm.1, s32[2,512,512]{2,1,0:T(8,128)} %flag_hbm.1), custom_call_target="tpu_custom_call" | custom-call | tf_op jit(solution)/shard_map/pallas_call | solution.py:730
  52.8 2.0 %shard_map.42 = (f32[2,512,512]{2,1,0:T(8,128)}, f32[2,512,512]{2,1,0:T(8,128)}) custom-call(f32[2,512,512]{2,1,0:T(8,128)S(1)} %get-tuple-element.4.sol_ref, f32[2,512,512]{2,1,0:T(8,128)S(1)} %get-tuple-element.5.res_ref), custom_call_target="tpu_custom_call" | custom-call | tf_op jit(solution)/shard_map/pallas_call | solution.py:763

commit v6 on v5

--- a/solution.py
+++ b/solution.py
@@ -20,7 +20,7 @@
 def kernel(
     count, chunk, stages,
     side_hbm, flag_hbm, sol_ref, res_ref,
-    rhs, flags, r0, inv, shadow, u0, u1, w0, w1, halo_r, halo_u, solid, fluid, code,
+    rhs, flags, r0, inv, shadow, u0, u1, w0, w1, halo_r, halo_u, solid, halves, fluid, code,
     pair, mine, got,
     in_sem, go, clear, known, bit_send, bit_recv, far_send, far_recv, near_send, near_recv,
     pair_send, pair_recv, sum_send, sum_recv,
@@ -29,7 +29,9 @@
     words = rows // 32
     steps = rows // TILE
     parts = rows // chunk
-    marks = sorted({0, 1, max(parts - 3, 0), max(parts - 2, 0), max(parts - 1, 0), parts})
+    marks = sorted({0, 1, parts // 2, max(parts - 2, 0), max(parts - 1, 0), parts})
+    plain = marks.index(parts // 2)
+    half = words // 2
     spans = [(a * chunk, (b - a) * chunk) for a, b in zip(marks, marks[1:])]
     most = (0, rows - spans[-1][1])
     late_marks = [rows * eighth // 8 for eighth in LATE]
@@ -122,6 +124,7 @@
     def _():
         solid[far_side * (depth + 2)] = jnp.zeros((words, cols), jnp.int32)
         solid[far_side * (depth + 2) + 1] = jnp.zeros((words, cols), jnp.int32)
+        halves[1] = jnp.zeros((half, cols), jnp.int32)
 
         def clear(t, carry):
             at = pl.ds(pl.multiple_of(t * TILE, TILE), TILE)
@@ -196,16 +199,26 @@
 
         on(far_side, some)
 
-    def bit_copy(side, depth_in=0, arrival=False):
-        mine_at = 2 + side * (depth - 1) + depth_in * (1 - 2 * side)
-        theirs_at = 1 + (1 - side) * (depth + 1) + depth_in * (1 - 2 * side)
-        halo_at = 1 + side * (depth + 1) - depth_in * (1 - 2 * side)
+    def bit_copy(side, arrival=False):
+        halo_at = 1 + side * (depth + 1)
+        source = halo_at if arrival else 2 + side * (depth - 1)
+        target = halo_at if arrival else 1 + (1 - side) * (depth + 1)
         return pltpu.make_async_remote_copy(
-            src_ref=solid.at[halo_at if arrival else mine_at],
-            dst_ref=solid.at[halo_at if arrival else theirs_at],
-            send_sem=bit_send,
-            recv_sem=bit_recv.at[2 if depth_in else side if arrival else 1 - side],
+            src_ref=solid.at[source],
+            dst_ref=solid.at[target],
+            send_sem=bit_send.at[0],
+            recv_sem=bit_recv.at[side if arrival else 1 - side],
             device_id=(me - 1 + 2 * side,),
+            device_id_type=MESH,
+        )
+
+    def half_copy(arrival=False):
+        return pltpu.make_async_remote_copy(
+            src_ref=halves.at[1 if arrival else 0],
+            dst_ref=halves.at[1],
+            send_sem=bit_send.at[1],
+            recv_sem=bit_recv.at[2],
+            device_id=(me - 1 + 2 * far_side,),
             device_id_type=MESH,
         )
 
@@ -214,7 +227,7 @@
         pltpu.make_async_remote_copy(
             src_ref=several,
             dst_ref=several,
-            send_sem=bit_send,
+            send_sem=bit_send.at[0],
             recv_sem=bit_recv.at[0],
             device_id=(partner,),
             device_id_type=MESH,
@@ -264,7 +277,9 @@
 
     @pl.when(is_even)
     def _():
-        on(far_side, lambda: bit_copy(0, 1).start())
+        low, high = solid[3, 0:half, :], solid[3, half:words, :]
+        halves[0] = jnp.bitwise_and(low, 0xFFFF) | jnp.left_shift(high, 16)
+        on(far_side, lambda: half_copy().start())
 
     @pl.when(is_odd)
     def _():
@@ -278,18 +293,14 @@
 
     @pl.when(is_even)
     def _():
-        far_pieces(1, kept, raw=True)
-
-        @pl.when(jnp.logical_not(is_first))
-        def _():
-            far_pieces(kept, len(spans), raw=True)
+        far_pieces(1, plain, raw=True)
 
     for plane in [near_plane] + inner_planes:
         load(plane, 1).wait()
         mask(plane, 0, steps)
 
-    bit_copy(near_side, 0, True).wait_recv()
-    on(far_side, lambda: bit_copy(far_side, 0, True).wait_recv())
+    bit_copy(near_side, True).wait_recv()
+    on(far_side, lambda: bit_copy(far_side, True).wait_recv())
 
     def classify(at, slot, known_fluid):
         word = solid[at]
@@ -365,29 +376,37 @@
     moment0 = lax.fori_loop(0, 32, first, none)
     near_copy(0).start()
 
+    @pl.when(is_even)
+    def _():
+        far_pieces(plain, kept)
+
+        @pl.when(jnp.logical_not(is_first))
+        def _():
+            far_pieces(kept, len(spans))
+
     @pl.when(jnp.logical_and(is_odd, is_first))
     def _():
         far_pieces(0, len(spans))
 
-    @pl.when(is_even)
-    def _():
-        def plain(t, carry):
-            at = pl.ds(pl.multiple_of(t * TILE, TILE), TILE)
-            shadow[at, :] = jnp.ones((TILE, cols), jnp.float32)
-            return carry
-
-        lax.fori_loop(0, steps, plain, 0)
+    def known_scale(t, carry):
+        at = pl.ds(pl.multiple_of(t * TILE, TILE), TILE)
+        shadow[at, :] = jnp.ones((TILE, cols), jnp.float32)
+        return carry
+
+    lax.fori_loop(odd * (steps // 2), steps, known_scale, 0)
 
     @pl.when(is_odd)
     def _():
-        on(far_side, lambda: bit_copy(1, 1, True).wait_recv())
+        on(far_side, lambda: half_copy(True).wait_recv())
+        solid[depth + 3, 0:half, :] = jnp.bitwise_and(halves[1], 0xFFFF)
+        solid[depth + 3, half:words, :] = lax.shift_right_logical(halves[1], 16)
         classify(depth + 2, depth, None)
 
         def beyond(j, carry):
             shadow[pl.ds(pl.multiple_of(j * words, words), words), :] = inverse(depth, j)
             return carry
 
-        lax.fori_loop(0, 32, beyond, 0)
+        lax.fori_loop(0, 16, beyond, 0)
         if rounds:
             hear(0)
 
@@ -445,7 +464,7 @@
 
     @pl.when(jnp.logical_and(is_even, is_first))
     def _():
-        far_pieces(kept, len(spans), raw=True)
+        far_pieces(kept, len(spans))
 
     @pl.when(jnp.logical_not(is_first))
     def _():
@@ -632,8 +651,9 @@
 
     @pl.when(is_even)
     def _():
-        pl.when(has_far)(lambda: bits_sent(3))
+        pl.when(has_far)(lambda: bits_sent(2))
         pl.when(jnp.logical_not(has_far))(lambda: bits_sent(1))
+        on(far_side, lambda: half_copy().wait_send())
         pl.when(is_first)(lambda: far_sent(0))
         sums(0, near_size).wait_send()
         sums(1, far_size).wait_recv()
@@ -720,8 +740,8 @@
     stages = groups(count // 2)
     widest = max(stages[0][0], stages[1][0], 2 * (stages[1][0] - 1))
     chunk = math.gcd(rows, CHUNK)
-    assert rows % (8 * TILE) == 0
-    pieces = max(len({0, 1, *(max(rows // chunk - i, 0) for i in range(4))}), len(LATE)) - 1
+    assert rows % 512 == 0
+    pieces = max(6, len(LATE)) - 1
     f32 = jnp.float32
     field = pltpu.VMEM((depth, rows, cols), f32)
     padded = pltpu.VMEM((depth, rows + 2 * PAD, cols), f32)
@@ -741,6 +761,7 @@
             pltpu.VMEM((2, rows, cols), f32),
             pltpu.VMEM((2, rows, cols), f32),
             pltpu.VMEM((depth + 4, rows // 32, cols), jnp.int32),
+            pltpu.VMEM((2, rows // 64, cols), jnp.int32),
             pltpu.VMEM((depth, rows // 32, cols), jnp.int32),
             pltpu.VMEM((depth + 1, 3, rows // 32, cols), jnp.int32),
             pltpu.VMEM((8, 128), f32),
@@ -750,7 +771,7 @@
             pltpu.SemaphoreType.REGULAR,
             pltpu.SemaphoreType.REGULAR,
             pltpu.SemaphoreType.REGULAR((max((stages[1][0] - 1).bit_length(), 1),)),
-            dma, dma((3,)),
+            dma((2,)), dma((3,)),
             dma((1 + len(LATE),)), dma((2, pieces)), dma((2,)), dma((2,)),
             dma, dma,
             dma((3,)), dma((2,)),

time: 55 us -> 54.8 us (level)
  no operation moved by 1% of the time
where the time goes in v6:
time: 54.8 us; the launch traced here: 54.7 us
  Pallas kernels  54.1 us (99%)
  between operations  0.64 us (1%)
    pallas_call x1, Pallas kernels, body(): pl.pallas_call(functools.partial(kernel, count, chunk, stages), out_shape...  52 us
    pallas_call x1, Pallas kernels, body(): pl.pallas_call(store, out_shape=(result, result), in_specs=[pl.BlockSpec(...  2.04 us

profile of v6, /device:TPU:1, one launch (start us, length us, event | category | flops | bytes accessed | tf_op | source)
XLA Modules:
  0.0 54.7 jit_solution(13459130545136611059)
XLA Ops:
  0.6 52.0 %shard_map.41 = (f32[2,512,512]{2,1,0:T(8,128)S(1)}, f32[2,512,512]{2,1,0:T(8,128)S(1)}) custom-call(f32[2,512,512]{2,1,0:T(8,128)} %side_hbm.1, s32[2,512,512]{2,1,0:T(8,128)} %flag_hbm.1), custom_call_target="tpu_custom_call" | custom-call | tf_op jit(solution)/shard_map/pallas_call | solution.py:750
  52.7 2.0 %shard_map.42 = (f32[2,512,512]{2,1,0:T(8,128)}, f32[2,512,512]{2,1,0:T(8,128)}) custom-call(f32[2,512,512]{2,1,0:T(8,128)S(1)} %get-tuple-element.4.sol_ref, f32[2,512,512]{2,1,0:T(8,128)S(1)} %get-tuple-element.5.res_ref), custom_call_target="tpu_custom_call" | custom-call | tf_op jit(solution)/shard_map/pallas_call | solution.py:784

commit v7 on v6

--- a/solution.py
+++ b/solution.py
@@ -703,12 +703,12 @@
             halo_arrival(1, 1, span, far_recv.at[1, i]).wait_recv()
 
             def tile(t, carry, span=span):
-                at = pl.ds(pl.multiple_of(span[0] + t * TILE, TILE), TILE)
+                at = pl.ds(pl.multiple_of(span[0] + t * final, final), final)
                 beyond = jnp.where(inv[plane, at, :] > 0.0, halo_u[1, at, :], 0.0)
                 res_ref[plane, at, :] = res_ref[plane, at, :] - trail * beyond
                 return carry
 
-            lax.fori_loop(0, span[1] // TILE, tile, 0)
+            lax.fori_loop(0, span[1] // final, tile, 0)
 
     @pl.when(jnp.logical_and(is_even, has_far))
     def _():
@@ -721,12 +721,12 @@
     for which, (source, target) in enumerate(((sol_ref, sol_out), (res_ref, res_out))):
         for plane in range(sol_ref.shape[0]):
             copies.append(
-                pltpu.make_async_copy(source.at[plane], target.at[plane], sem.at[which, plane])
+                pltpu.make_async_copy(source.at[plane], target.at[plane], sem.at[which])
             )
     for copy in copies:
         copy.start()
-    for copy in copies:
-        copy.wait()
+    for which, (source, target) in enumerate(((sol_ref, sol_out), (res_ref, res_out))):
+        pltpu.make_async_copy(source, target, sem.at[which]).wait()
 
 
 def groups(chips):
@@ -786,7 +786,7 @@
         out_shape=(result, result),
         in_specs=[pl.BlockSpec(memory_space=pltpu.VMEM)] * 2,
         out_specs=(pl.BlockSpec(memory_space=pltpu.HBM),) * 2,
-        scratch_shapes=[dma((2, depth))],
+        scratch_shapes=[dma((2,))],
         compiler_params=pltpu.CompilerParams(vmem_limit_bytes=2**19),
     )(*fields)
 

time: 54.8 us -> 54.8 us (level)
  no operation moved by 1% of the time
where the time goes in v7:
time: 54.8 us; the launch traced here: 54.7 us
  Pallas kernels  54 us (99%)
  between operations  0.64 us (1%)
    pallas_call x1, Pallas kernels, body(): pl.pallas_call(functools.partial(kernel, count, chunk, stages), out_shape...  52 us
    pallas_call x1, Pallas kernels, body(): pl.pallas_call(store, out_shape=(result, result), in_specs=[pl.BlockSpec(...  2.03 us

profile of v7, /device:TPU:1, one launch (start us, length us, event | category | flops | bytes accessed | tf_op | source)
XLA Modules:
  0.0 54.7 jit_solution(15139760398780855391)
XLA Ops:
  0.6 52.0 %shard_map.41 = (f32[2,512,512]{2,1,0:T(8,128)S(1)}, f32[2,512,512]{2,1,0:T(8,128)S(1)}) custom-call(f32[2,512,512]{2,1,0:T(8,128)} %side_hbm.1, s32[2,512,512]{2,1,0:T(8,128)} %flag_hbm.1), custom_call_target="tpu_custom_call" | custom-call | tf_op jit(solution)/shard_map/pallas_call | solution.py:750
  52.6 2.0 %shard_map.42 = (f32[2,512,512]{2,1,0:T(8,128)}, f32[2,512,512]{2,1,0:T(8,128)}) custom-call(f32[2,512,512]{2,1,0:T(8,128)S(1)} %get-tuple-element.4.sol_ref, f32[2,512,512]{2,1,0:T(8,128)S(1)} %get-tuple-element.5.res_ref), custom_call_target="tpu_custom_call" | custom-call | tf_op jit(solution)/shard_map/pallas_call | solution.py:784

commit v8 on v7

--- a/solution.py
+++ b/solution.py
@@ -10,7 +10,7 @@
 
 MESH = pl.DeviceIdType.MESH
 TILE = 16
-LAST = 64
+LAST = 128
 LATE = (0, 2, 3, 5, 7, 8)
 CHUNK = 64
 PAD = 8
@@ -37,6 +37,7 @@
     late_marks = [rows * eighth // 8 for eighth in LATE]
     lates = [(a, b - a) for a, b in zip(late_marks, late_marks[1:])]
     final = math.gcd(rows, LAST)
+    late_rows = math.gcd(chunk, LAST)
     near_size, far_size = stages[0][0], stages[1][0]
     me = lax.axis_index("gz")
     chip, odd = me // 2, lax.rem(me, 2)
@@ -703,12 +704,12 @@
             halo_arrival(1, 1, span, far_recv.at[1, i]).wait_recv()
 
             def tile(t, carry, span=span):
-                at = pl.ds(pl.multiple_of(span[0] + t * final, final), final)
+                at = pl.ds(pl.multiple_of(span[0] + t * late_rows, late_rows), late_rows)
                 beyond = jnp.where(inv[plane, at, :] > 0.0, halo_u[1, at, :], 0.0)
                 res_ref[plane, at, :] = res_ref[plane, at, :] - trail * beyond
                 return carry
 
-            lax.fori_loop(0, span[1] // final, tile, 0)
+            lax.fori_loop(0, span[1] // late_rows, tile, 0)
 
     @pl.when(jnp.logical_and(is_even, has_far))
     def _():

time: 54.8 us -> 54.8 us (level)
  no operation moved by 1% of the time
where the time goes in v8:
time: 54.8 us; the launch traced here: 54.7 us
  Pallas kernels  54 us (99%)
  between operations  0.64 us (1%)
    pallas_call x1, Pallas kernels, body(): pl.pallas_call(functools.partial(kernel, count, chunk, stages), out_shape...  52 us
    pallas_call x1, Pallas kernels, body(): pl.pallas_call(store, out_shape=(result, result), in_specs=[pl.BlockSpec(...  2.03 us

profile of v8, /device:TPU:1, one launch (start us, length us, event | category | flops | bytes accessed | tf_op | source)
XLA Modules:
  0.0 54.7 jit_solution(16717974040318832248)
XLA Ops:
  0.6 52.0 %shard_map.41 = (f32[2,512,512]{2,1,0:T(8,128)S(1)}, f32[2,512,512]{2,1,0:T(8,128)S(1)}) custom-call(f32[2,512,512]{2,1,0:T(8,128)} %side_hbm.1, s32[2,512,512]{2,1,0:T(8,128)} %flag_hbm.1), custom_call_target="tpu_custom_call" | custom-call | tf_op jit(solution)/shard_map/pallas_call | solution.py:751
  52.6 2.0 %shard_map.42 = (f32[2,512,512]{2,1,0:T(8,128)}, f32[2,512,512]{2,1,0:T(8,128)}) custom-call(f32[2,512,512]{2,1,0:T(8,128)S(1)} %get-tuple-element.4.sol_ref, f32[2,512,512]{2,1,0:T(8,128)S(1)} %get-tuple-element.5.res_ref), custom_call_target="tpu_custom_call" | custom-call | tf_op jit(solution)/shard_map/pallas_call | solution.py:785
